TPU v7x, 32 devices: a whole 2x2x4 slice. The times are simulated.
32 devices in a mesh: dp: 2 (over x), tp: 4 (over z), pp: 4 (over y, core).
Axes of the slice: x: 2, y: 2, z: 4, core: 2. Of those that a mesh axis runs over, the one named last changes fastest.
Arguments:
- x_in: bfloat16 [8, 1, 128, 2560], P('dp'), parts along dimension 0
- seq_lens: int32 [8, 1], P('dp'), parts along dimension 0
- ln1_gain: bfloat16 [4, 2560], P('pp')
- ln1_shift: bfloat16 [4, 2560], P('pp')
- w_qkv: bfloat16 [4, 2560, 3, 2560], P('pp', None, None, 'tp')
- b_qkv: bfloat16 [4, 3, 32, 80], P('pp', None, 'tp')
- w_out: bfloat16 [4, 2560, 2560], P('pp', 'tp')
- b_out: bfloat16 [4, 2560], P('pp')
- ln2_gain: bfloat16 [4, 2560], P('pp')
- ln2_shift: bfloat16 [4, 2560], P('pp')
- w_up: bfloat16 [4, 2560, 10240], P('pp', None, 'tp')
- b_up: bfloat16 [4, 10240], P('pp', 'tp')
- w_down: bfloat16 [4, 10240, 2560], P('pp', 'tp')
- b_down: bfloat16 [4, 2560], P('pp')
Outputs:
- output: bfloat16 [4, 8, 1, 128, 2560], P('pp', 'dp'), parts along dimension 1
There are 2 independent parts. A program takes and returns all parts, laid end to end along the dimension named above; an argument that names none is the same for every part.
All inputs are finite; a program needn't handle non-finite values.
Results may differ from a plain program's by a relative error of at most 0.0189996.
Values are sent between devices in bfloat16 or wider.
A program may use at most 1 GiB of HBM per device.

v0:
```python
import jax
import jax.numpy as jnp
from jax import lax
from jax.sharding import PartitionSpec as P
import math


def alibi_slopes(heads_n):
    closest = 2 ** int(math.floor(math.log2(heads_n)))
    base_rate = 2.0 ** (-8.0 / closest)
    slope_list = [base_rate ** (head_idx + 1) for head_idx in range(closest)]
    extra_rate = 2.0 ** (-4.0 / closest)
    slope_list = slope_list + [extra_rate ** (2 * head_idx + 1) for head_idx in range(min(closest, heads_n - closest))]
    return jnp.array(slope_list, dtype=jnp.float32)


def layer_norm(values, gain_vec, shift_vec):
    val_f = values.astype(jnp.float32)
    mean_val = jnp.mean(val_f, axis=-1, keepdims=True)
    centered = val_f - mean_val
    var_val = jnp.mean(centered * centered, axis=-1, keepdims=True)
    normed = centered * lax.rsqrt(var_val + 1e-5)
    return (normed * gain_vec.astype(jnp.float32) + shift_vec.astype(jnp.float32)).astype(jnp.bfloat16)


def attention(query_all, key_all, val_all, slopes, lens_row):
    batch_n, seq_n, heads_n, head_dim = query_all.shape
    blk_len = min(seq_n, 128)
    key_pos = jnp.arange(seq_n)
    key_ok = key_pos[None, :] < lens_row[:, None]

    def one_block(blk_idx):
        query_blk = lax.dynamic_slice_in_dim(query_all, blk_idx * blk_len, blk_len, 1)
        scores = jnp.einsum('bqhe,bkhe->bhqk', query_blk, key_all, preferred_element_type=jnp.float32) * (head_dim ** -0.5)
        query_pos = blk_idx * blk_len + jnp.arange(blk_len)
        distance = (query_pos[:, None] - key_pos[None, :]).astype(jnp.float32)
        scores = scores - slopes[None, :, None, None] * distance[None, None]
        allowed = (key_pos[None, :] <= query_pos[:, None])[None, None] & key_ok[:, None, None, :]
        scores = jnp.where(allowed, scores, -1e30)
        prob_bf = jax.nn.softmax(scores, axis=-1).astype(jnp.bfloat16)
        return jnp.einsum('bhqk,bkhe->bqhe', prob_bf, val_all, preferred_element_type=jnp.float32).astype(jnp.bfloat16)

    return lax.map(one_block, jnp.arange(seq_n // blk_len))


def stage_layer(act_in, lens_row, layer_w, slopes):
    ln1_gain, ln1_shift, w_qkv, b_qkv, w_out, b_out, ln2_gain, ln2_shift, w_up, b_up, w_down, b_down = layer_w
    batch_n, seq_n, model_n = act_in.shape
    tokens_n = batch_n * seq_n
    heads_loc, head_dim = b_qkv.shape[1], b_qkv.shape[2]
    width_loc = heads_loc * head_dim
    flat_in = act_in.reshape(tokens_n, model_n)
    normed = layer_norm(flat_in, ln1_gain, ln1_shift)
    qkv_loc = (jnp.dot(normed, w_qkv.reshape(model_n, 3 * width_loc), preferred_element_type=jnp.float32) + b_qkv.reshape(3 * width_loc).astype(jnp.float32)).astype(jnp.bfloat16)
    qkv_loc = qkv_loc.reshape(batch_n, seq_n, 3, heads_loc, head_dim)
    ctx_blocks = attention(qkv_loc[:, :, 0], qkv_loc[:, :, 1], qkv_loc[:, :, 2], slopes, lens_row)
    attn_part = jnp.einsum('nbqhe,hef->bnqf', ctx_blocks, w_out.reshape(heads_loc, head_dim, model_n), preferred_element_type=jnp.float32).astype(jnp.bfloat16)
    attn_sum = lax.psum(attn_part.reshape(tokens_n, model_n), 'tp')
    resid_act = (flat_in.astype(jnp.float32) + attn_sum.astype(jnp.float32) + b_out.astype(jnp.float32)).astype(jnp.bfloat16)
    normed_mlp = layer_norm(resid_act, ln2_gain, ln2_shift)
    hidden_act = jax.nn.gelu(jnp.dot(normed_mlp, w_up, preferred_element_type=jnp.float32) + b_up.astype(jnp.float32), approximate=True).astype(jnp.bfloat16)
    mlp_part = jnp.dot(hidden_act, w_down, preferred_element_type=jnp.float32).astype(jnp.bfloat16)
    mlp_sum = lax.psum(mlp_part, 'tp')
    result = (resid_act.astype(jnp.float32) + mlp_sum.astype(jnp.float32) + b_down.astype(jnp.float32)).astype(jnp.bfloat16)
    return result.reshape(batch_n, seq_n, model_n)


def solution(mesh):
    stages = mesh.shape['pp']
    tp_size = mesh.shape['tp']
    next_pairs = [(src_stage, src_stage + 1) for src_stage in range(stages - 1)]
    in_specs = (P('dp'), P('dp'), P('pp'), P('pp'), P('pp', None, None, 'tp'), P('pp', None, 'tp', None), P('pp', 'tp', None), P('pp'), P('pp'), P('pp'), P('pp', None, 'tp'), P('pp', 'tp'), P('pp', 'tp', None), P('pp'))

    def per_device(x_in, seq_lens, ln1_gain, ln1_shift, w_qkv, b_qkv, w_out, b_out, ln2_gain, ln2_shift, w_up, b_up, w_down, b_down):
        stage_idx = lax.axis_index('pp')
        tp_rank = lax.axis_index('tp')
        layer_w = tuple(stacked[0] for stacked in (ln1_gain, ln1_shift, w_qkv, b_qkv, w_out, b_out, ln2_gain, ln2_shift, w_up, b_up, w_down, b_down))
        heads_loc = b_qkv.shape[2]
        slopes = lax.dynamic_slice_in_dim(alibi_slopes(heads_loc * tp_size), tp_rank * heads_loc, heads_loc)
        micro_n = x_in.shape[0]

        def one_step(time_idx, loop_state):
            received, outputs = loop_state
            first_in = lax.dynamic_index_in_dim(x_in, jnp.minimum(time_idx, micro_n - 1), 0, keepdims=False)
            act_in = jnp.where(stage_idx == 0, first_in, received)
            micro_idx = jnp.clip(time_idx - stage_idx, 0, micro_n - 1)
            lens_row = lax.dynamic_index_in_dim(seq_lens, micro_idx, 0, keepdims=False)
            act_out = stage_layer(act_in, lens_row, layer_w, slopes)
            active = (time_idx >= stage_idx) & (time_idx - stage_idx < micro_n)
            previous = lax.dynamic_index_in_dim(outputs, micro_idx, 0, keepdims=False)
            outputs = lax.dynamic_update_index_in_dim(outputs, jnp.where(active, act_out, previous), micro_idx, 0)
            received = lax.ppermute(act_out, 'pp', next_pairs)
            return received, outputs

        loop_init = (jnp.zeros(x_in.shape[1:], x_in.dtype), jnp.zeros(x_in.shape, x_in.dtype))
        last_recv, outputs = lax.fori_loop(0, micro_n + stages - 1, one_step, loop_init)
        return outputs[None]

    return jax.shard_map(per_device, mesh=mesh, in_specs=in_specs, out_specs=P('pp', 'dp'), check_vma=False)
```

profile of v0, /device:TPU:5, one launch (start us, length us, event | category | flops | bytes accessed | tf_op | source)
XLA Modules:
  0.0 892.7 jit_solution(9795366517994689979)
XLA Ops:
  7.3 13.8 %copy.22 = bf16[1,2560,3,640]{1,3,2,0:T(8,128)(2,1)} copy(bf16[1,2560,3,640]{3,1,2,0:T(8,128)(2,1)} %param.21) | data formatting | bytes 19660800 | tf_op jit(solution)/shard_map/while | solution.py:96
  23.3 862.9 %while.25 = (s32[]{:T(128)}, bf16[1,128,2560]{2,1,0:T(8,128)(2,1)S(1)}, bf16[4,1,128,2560]{3,2,1,0:T(8,128)(2,1)}, pred[]{:T(512)}, bf16[4,1,128,2560]{3,2,1,0:T...) while((s32[]{:T(128)}, ...), condition=%wide.region_9.10_spmd, body=%wide.region_0.9_spmd.sunk | while | flops 5116464128 | bytes 70531568 | solution.py:96
  25.2 7.1 fusion.90
  34.5 3.7 fusion.93
  38.4 41.5 %all-reduce.3.cloned.1.call-done = bf16[128,2560]{1,0:T(8,128)(2,1)} async-done(((bf16[128,2560]{1,0:T(8,128)(2,1)}), bf16[128,2560]{1,0:T(8,128)(2,1)}) %all-reduce.3.cloned.1.call-update) | async-done | bytes 655376 | tf_op jit(solution)/shard_map/while/body/eval_jaxpr/psum | solution.py:58
  81.6 13.3 %convolution_convert_fusion.3 = bf16[128,2560]{1,0:T(8,128)(2,1)} fusion(bf16[2560,2560]{1,0:T(8,128)(2,1)} %get-tuple-element.751, bf16[2560,2560]{1,0:T(8,128)(2,1)} %get-tuple-element.749, bf16[128,2560]{1,0:T(8,128)(2,1)S(1)} %get-tuple-element.683, f32[2560]{0:T(1024)S(1)} %convert_element_type.446, f32[2560]{0:T(1024)S(1)} %convert_element_type.447, ...), kind=kOutput, calls=%fused_computation.4.clone.1 | convolution fusion | flops 3361013760 | bytes 27556864 | tf_op jit(solution)/shard_map/while/body/eval_jaxpr/dot_general | solution.py:62
  96.2 39.3 %all-reduce.5.cloned.1.call-done = bf16[128,2560]{1,0:T(8,128)(2,1)} async-done(((bf16[128,2560]{1,0:T(8,128)(2,1)}), bf16[128,2560]{1,0:T(8,128)(2,1)}) %all-reduce.5.cloned.1.call-update) | async-done | bytes 655376 | tf_op jit(solution)/shard_map/while/body/eval_jaxpr/psum | solution.py:63
  143.3 7.1 fusion.90
  156.4 47.6 %all-reduce.3.cloned.1.call-done = bf16[128,2560]{1,0:T(8,128)(2,1)} async-done(((bf16[128,2560]{1,0:T(8,128)(2,1)}), bf16[128,2560]{1,0:T(8,128)(2,1)}) %all-reduce.3.cloned.1.call-update) | async-done | bytes 655376 | tf_op jit(solution)/shard_map/while/body/eval_jaxpr/psum | solution.py:58
  205.8 13.3 %convolution_convert_fusion.3 = bf16[128,2560]{1,0:T(8,128)(2,1)} fusion(bf16[2560,2560]{1,0:T(8,128)(2,1)} %get-tuple-element.751, bf16[2560,2560]{1,0:T(8,128)(2,1)} %get-tuple-element.749, bf16[128,2560]{1,0:T(8,128)(2,1)S(1)} %get-tuple-element.683, f32[2560]{0:T(1024)S(1)} %convert_element_type.446, f32[2560]{0:T(1024)S(1)} %convert_element_type.447, ...), kind=kOutput, calls=%fused_computation.4.clone.1 | convolution fusion | flops 3361013760 | bytes 27556864 | tf_op jit(solution)/shard_map/while/body/eval_jaxpr/dot_general | solution.py:62
  220.3 39.3 %all-reduce.5.cloned.1.call-done = bf16[128,2560]{1,0:T(8,128)(2,1)} async-done(((bf16[128,2560]{1,0:T(8,128)(2,1)}), bf16[128,2560]{1,0:T(8,128)(2,1)}) %all-reduce.5.cloned.1.call-update) | async-done | bytes 655376 | tf_op jit(solution)/shard_map/while/body/eval_jaxpr/psum | solution.py:63
  267.4 7.1 fusion.90
  280.6 47.6 %all-reduce.3.cloned.1.call-done = bf16[128,2560]{1,0:T(8,128)(2,1)} async-done(((bf16[128,2560]{1,0:T(8,128)(2,1)}), bf16[128,2560]{1,0:T(8,128)(2,1)}) %all-reduce.3.cloned.1.call-update) | async-done | bytes 655376 | tf_op jit(solution)/shard_map/while/body/eval_jaxpr/psum | solution.py:58
  329.9 13.3 %convolution_convert_fusion.3 = bf16[128,2560]{1,0:T(8,128)(2,1)} fusion(bf16[2560,2560]{1,0:T(8,128)(2,1)} %get-tuple-element.751, bf16[2560,2560]{1,0:T(8,128)(2,1)} %get-tuple-element.749, bf16[128,2560]{1,0:T(8,128)(2,1)S(1)} %get-tuple-element.683, f32[2560]{0:T(1024)S(1)} %convert_element_type.446, f32[2560]{0:T(1024)S(1)} %convert_element_type.447, ...), kind=kOutput, calls=%fused_computation.4.clone.1 | convolution fusion | flops 3361013760 | bytes 27556864 | tf_op jit(solution)/shard_map/while/body/eval_jaxpr/dot_general | solution.py:62
  344.4 39.3 %all-reduce.5.cloned.1.call-done = bf16[128,2560]{1,0:T(8,128)(2,1)} async-done(((bf16[128,2560]{1,0:T(8,128)(2,1)}), bf16[128,2560]{1,0:T(8,128)(2,1)}) %all-reduce.5.cloned.1.call-update) | async-done | bytes 655376 | tf_op jit(solution)/shard_map/while/body/eval_jaxpr/psum | solution.py:63
  391.5 7.1 fusion.90
  404.7 47.6 %all-reduce.3.cloned.1.call-done = bf16[128,2560]{1,0:T(8,128)(2,1)} async-done(((bf16[128,2560]{1,0:T(8,128)(2,1)}), bf16[128,2560]{1,0:T(8,128)(2,1)}) %all-reduce.3.cloned.1.call-update) | async-done | bytes 655376 | tf_op jit(solution)/shard_map/while/body/eval_jaxpr/psum | solution.py:58
  454.0 13.3 %convolution_convert_fusion.3 = bf16[128,2560]{1,0:T(8,128)(2,1)} fusion(bf16[2560,2560]{1,0:T(8,128)(2,1)} %get-tuple-element.751, bf16[2560,2560]{1,0:T(8,128)(2,1)} %get-tuple-element.749, bf16[128,2560]{1,0:T(8,128)(2,1)S(1)} %get-tuple-element.683, f32[2560]{0:T(1024)S(1)} %convert_element_type.446, f32[2560]{0:T(1024)S(1)} %convert_element_type.447, ...), kind=kOutput, calls=%fused_computation.4.clone.1 | convolution fusion | flops 3361013760 | bytes 27556864 | tf_op jit(solution)/shard_map/while/body/eval_jaxpr/dot_general | solution.py:62
  468.6 39.3 %all-reduce.5.cloned.1.call-done = bf16[128,2560]{1,0:T(8,128)(2,1)} async-done(((bf16[128,2560]{1,0:T(8,128)(2,1)}), bf16[128,2560]{1,0:T(8,128)(2,1)}) %all-reduce.5.cloned.1.call-update) | async-done | bytes 655376 | tf_op jit(solution)/shard_map/while/body/eval_jaxpr/psum | solution.py:63
  515.7 7.1 fusion.90
  528.8 47.6 %all-reduce.3.cloned.1.call-done = bf16[128,2560]{1,0:T(8,128)(2,1)} async-done(((bf16[128,2560]{1,0:T(8,128)(2,1)}), bf16[128,2560]{1,0:T(8,128)(2,1)}) %all-reduce.3.cloned.1.call-update) | async-done | bytes 655376 | tf_op jit(solution)/shard_map/while/body/eval_jaxpr/psum | solution.py:58
  578.1 13.3 %convolution_convert_fusion.3 = bf16[128,2560]{1,0:T(8,128)(2,1)} fusion(bf16[2560,2560]{1,0:T(8,128)(2,1)} %get-tuple-element.751, bf16[2560,2560]{1,0:T(8,128)(2,1)} %get-tuple-element.749, bf16[128,2560]{1,0:T(8,128)(2,1)S(1)} %get-tuple-element.683, f32[2560]{0:T(1024)S(1)} %convert_element_type.446, f32[2560]{0:T(1024)S(1)} %convert_element_type.447, ...), kind=kOutput, calls=%fused_computation.4.clone.1 | convolution fusion | flops 3361013760 | bytes 27556864 | tf_op jit(solution)/shard_map/while/body/eval_jaxpr/dot_general | solution.py:62
  592.7 39.3 %all-reduce.5.cloned.1.call-done = bf16[128,2560]{1,0:T(8,128)(2,1)} async-done(((bf16[128,2560]{1,0:T(8,128)(2,1)}), bf16[128,2560]{1,0:T(8,128)(2,1)}) %all-reduce.5.cloned.1.call-update) | async-done | bytes 655376 | tf_op jit(solution)/shard_map/while/body/eval_jaxpr/psum | solution.py:63
  639.8 7.1 fusion.90
  649.1 3.7 fusion.93
  652.9 47.6 %all-reduce.3.cloned.1.call-done = bf16[128,2560]{1,0:T(8,128)(2,1)} async-done(((bf16[128,2560]{1,0:T(8,128)(2,1)}), bf16[128,2560]{1,0:T(8,128)(2,1)}) %all-reduce.3.cloned.1.call-update) | async-done | bytes 655376 | tf_op jit(solution)/shard_map/while/body/eval_jaxpr/psum | solution.py:58
  702.3 13.3 %convolution_convert_fusion.3 = bf16[128,2560]{1,0:T(8,128)(2,1)} fusion(bf16[2560,2560]{1,0:T(8,128)(2,1)} %get-tuple-element.751, bf16[2560,2560]{1,0:T(8,128)(2,1)} %get-tuple-element.749, bf16[128,2560]{1,0:T(8,128)(2,1)S(1)} %get-tuple-element.683, f32[2560]{0:T(1024)S(1)} %convert_element_type.446, f32[2560]{0:T(1024)S(1)} %convert_element_type.447, ...), kind=kOutput, calls=%fused_computation.4.clone.1 | convolution fusion | flops 3361013760 | bytes 27556864 | tf_op jit(solution)/shard_map/while/body/eval_jaxpr/dot_general | solution.py:62
  716.8 39.3 %all-reduce.5.cloned.1.call-done = bf16[128,2560]{1,0:T(8,128)(2,1)} async-done(((bf16[128,2560]{1,0:T(8,128)(2,1)}), bf16[128,2560]{1,0:T(8,128)(2,1)}) %all-reduce.5.cloned.1.call-update) | async-done | bytes 655376 | tf_op jit(solution)/shard_map/while/body/eval_jaxpr/psum | solution.py:63
  763.9 7.1 fusion.90
  777.1 47.6 %all-reduce.3.cloned.1.call-done = bf16[128,2560]{1,0:T(8,128)(2,1)} async-done(((bf16[128,2560]{1,0:T(8,128)(2,1)}), bf16[128,2560]{1,0:T(8,128)(2,1)}) %all-reduce.3.cloned.1.call-update) | async-done | bytes 655376 | tf_op jit(solution)/shard_map/while/body/eval_jaxpr/psum | solution.py:58
  826.4 13.3 %convolution_convert_fusion.3 = bf16[128,2560]{1,0:T(8,128)(2,1)} fusion(bf16[2560,2560]{1,0:T(8,128)(2,1)} %get-tuple-element.751, bf16[2560,2560]{1,0:T(8,128)(2,1)} %get-tuple-element.749, bf16[128,2560]{1,0:T(8,128)(2,1)S(1)} %get-tuple-element.683, f32[2560]{0:T(1024)S(1)} %convert_element_type.446, f32[2560]{0:T(1024)S(1)} %convert_element_type.447, ...), kind=kOutput, calls=%fused_computation.4.clone.1 | convolution fusion | flops 3361013760 | bytes 27556864 | tf_op jit(solution)/shard_map/while/body/eval_jaxpr/dot_general | solution.py:62
  840.9 39.3 %all-reduce.5.cloned.1.call-done = bf16[128,2560]{1,0:T(8,128)(2,1)} async-done(((bf16[128,2560]{1,0:T(8,128)(2,1)}), bf16[128,2560]{1,0:T(8,128)(2,1)}) %all-reduce.5.cloned.1.call-update) | async-done | bytes 655376 | tf_op jit(solution)/shard_map/while/body/eval_jaxpr/psum | solution.py:63
  (271 shorter events, 112.2 us)
Async XLA Ops:
  7.3 13.9 %copy-start.2 = (bf16[1,2560]{1,0:T(2,128)(2,1)S(1)}, bf16[1,2560]{1,0:T(2,128)(2,1)}, u32[]{:S(2)}) copy-start(bf16[1,2560]{1,0:T(2,128)(2,1)} %param.19) | copy-start | bytes 15364
  7.3 13.9 %copy-start.3 = (bf16[1,2560]{1,0:T(2,128)(2,1)S(1)}, bf16[1,2560]{1,0:T(2,128)(2,1)}, u32[]{:S(2)}) copy-start(bf16[1,2560]{1,0:T(2,128)(2,1)} %param.20) | copy-start | bytes 15364
  7.3 14.0 %copy-start.4 = (bf16[1,2560]{1,0:T(2,128)(2,1)S(1)}, bf16[1,2560]{1,0:T(2,128)(2,1)}, u32[]{:S(2)}) copy-start(bf16[1,2560]{1,0:T(2,128)(2,1)} %param.24) | copy-start | bytes 15364
  7.3 14.0 %copy-start.5 = (bf16[1,2560]{1,0:T(2,128)(2,1)S(1)}, bf16[1,2560]{1,0:T(2,128)(2,1)}, u32[]{:S(2)}) copy-start(bf16[1,2560]{1,0:T(2,128)(2,1)} %param.25) | copy-start | bytes 15364
  7.3 14.1 %copy-start.6 = (bf16[1,2560]{1,0:T(2,128)(2,1)S(1)}, bf16[1,2560]{1,0:T(2,128)(2,1)}, u32[]{:S(2)}) copy-start(bf16[1,2560]{1,0:T(2,128)(2,1)} %param.26) | copy-start | bytes 15364
  7.3 14.1 %copy-start.7 = (bf16[1,2560]{1,0:T(2,128)(2,1)S(1)}, bf16[1,2560]{1,0:T(2,128)(2,1)}, u32[]{:S(2)}) copy-start(bf16[1,2560]{1,0:T(2,128)(2,1)} %param.28) | copy-start | bytes 15364
  7.3 14.2 %copy-start.8 = (bf16[1,2560]{1,0:T(2,128)(2,1)S(1)}, bf16[1,2560]{1,0:T(2,128)(2,1)}, u32[]{:S(2)}) copy-start(bf16[1,2560]{1,0:T(2,128)(2,1)} %param.30) | copy-start | bytes 15364
  23.3 56.6 %all-reduce.3.cloned.1.call-start = ((), (), s32[]{:S(2)}) async-start(), calls=%async_computation | async-start | bytes 1310720 | tf_op jit(solution)/shard_map/while/body/eval_jaxpr/psum | solution.py:58
  38.3 97.1 %all-reduce.5.cloned.1.call-start = ((), (), s32[]{:S(2)}) async-start(), calls=%async_computation.1 | async-start | bytes 1310720 | tf_op jit(solution)/shard_map/while/body/eval_jaxpr/psum | solution.py:63
  135.4 2.7 copy-start
  136.8 4.6 collective-permute-start
  141.4 62.6 %all-reduce.3.cloned.1.call-start = ((), (), s32[]{:S(2)}) async-start(), calls=%async_computation | async-start | bytes 1310720 | tf_op jit(solution)/shard_map/while/body/eval_jaxpr/psum | solution.py:58
  156.3 103.2 %all-reduce.5.cloned.1.call-start = ((), (), s32[]{:S(2)}) async-start(), calls=%async_computation.1 | async-start | bytes 1310720 | tf_op jit(solution)/shard_map/while/body/eval_jaxpr/psum | solution.py:63
  259.6 2.7 copy-start
  260.9 4.6 collective-permute-start
  265.6 62.6 %all-reduce.3.cloned.1.call-start = ((), (), s32[]{:S(2)}) async-start(), calls=%async_computation | async-start | bytes 1310720 | tf_op jit(solution)/shard_map/while/body/eval_jaxpr/psum | solution.py:58
  280.5 103.2 %all-reduce.5.cloned.1.call-start = ((), (), s32[]{:S(2)}) async-start(), calls=%async_computation.1 | async-start | bytes 1310720 | tf_op jit(solution)/shard_map/while/body/eval_jaxpr/psum | solution.py:63
  383.7 2.7 copy-start
  385.0 4.6 collective-permute-start
  389.7 62.6 %all-reduce.3.cloned.1.call-start = ((), (), s32[]{:S(2)}) async-start(), calls=%async_computation | async-start | bytes 1310720 | tf_op jit(solution)/shard_map/while/body/eval_jaxpr/psum | solution.py:58
  404.6 103.2 %all-reduce.5.cloned.1.call-start = ((), (), s32[]{:S(2)}) async-start(), calls=%async_computation.1 | async-start | bytes 1310720 | tf_op jit(solution)/shard_map/while/body/eval_jaxpr/psum | solution.py:63
  509.2 4.6 collective-permute-start
  513.8 62.6 %all-reduce.3.cloned.1.call-start = ((), (), s32[]{:S(2)}) async-start(), calls=%async_computation | async-start | bytes 1310720 | tf_op jit(solution)/shard_map/while/body/eval_jaxpr/psum | solution.py:58
  528.7 103.2 %all-reduce.5.cloned.1.call-start = ((), (), s32[]{:S(2)}) async-start(), calls=%async_computation.1 | async-start | bytes 1310720 | tf_op jit(solution)/shard_map/while/body/eval_jaxpr/psum | solution.py:63
  633.3 4.6 collective-permute-start
  637.9 62.6 %all-reduce.3.cloned.1.call-start = ((), (), s32[]{:S(2)}) async-start(), calls=%async_computation | async-start | bytes 1310720 | tf_op jit(solution)/shard_map/while/body/eval_jaxpr/psum | solution.py:58
  652.8 103.2 %all-reduce.5.cloned.1.call-start = ((), (), s32[]{:S(2)}) async-start(), calls=%async_computation.1 | async-start | bytes 1310720 | tf_op jit(solution)/shard_map/while/body/eval_jaxpr/psum | solution.py:63
  757.4 4.6 collective-permute-start
  762.1 62.6 %all-reduce.3.cloned.1.call-start = ((), (), s32[]{:S(2)}) async-start(), calls=%async_computation | async-start | bytes 1310720 | tf_op jit(solution)/shard_map/while/body/eval_jaxpr/psum | solution.py:58
  777.0 103.2 %all-reduce.5.cloned.1.call-start = ((), (), s32[]{:S(2)}) async-start(), calls=%async_computation.1 | async-start | bytes 1310720 | tf_op jit(solution)/shard_map/while/body/eval_jaxpr/psum | solution.py:63
  880.2 2.7 copy-start
  881.5 4.6 collective-permute-start
  (5 other events, 11.5 us)
Sparse Core Ops, SparseCore 0:
  38.4 41.4 all-reduce.2
  95.1 40.2 all-reduce.4
  156.5 47.5 all-reduce.2
  219.3 40.2 all-reduce.4
  280.6 47.5 all-reduce.2
  343.4 40.2 all-reduce.4
  404.7 47.5 all-reduce.2
  467.5 40.2 all-reduce.4
  528.8 47.5 all-reduce.2
  591.6 40.2 all-reduce.4
  653.0 47.5 all-reduce.2
  715.8 40.2 all-reduce.4
  777.1 47.5 all-reduce.2
  839.9 40.2 all-reduce.4
where the time goes:
time: 903 us; the launch traced here: 893 us
  waiting for transfers between devices  617 us (68%)
  matrix products  174 us (19%)
  other arithmetic  46.6 us (5%)
  local copies, waits for them, and re-layouts  31 us (3%)
  between operations  13.2 us (1%)
  starting transfers between devices  9.39 us (1%)
    psum x7, waiting for transfers between devices, stage_layer(): attn_sum = lax.psum(attn_part.reshape(tokens_n, model_n), 'tp')  327 us
    psum x7, waiting for transfers between devices, stage_layer(): mlp_sum = lax.psum(mlp_part, 'tp')  275 us
    dot_general x7, matrix products, stage_layer(): jnp.dot(hidden_act, w_down, preferred_element_type=jnp.float32)  93.4 us
    dot_general x7, matrix products, stage_layer(): jnp.dot(normed, w_qkv.reshape(model_n, 3 * width_loc), preferred_element_...  49.6 us
    dot_general x7, matrix products, stage_layer(): jnp.einsum('nbqhe,hef->bnqf', ctx_blocks, w_out.reshape(heads_loc, head_d...  26 us
    reduce_sum x14, other arithmetic, layer_norm(): mean_val = jnp.mean(val_f, axis=-1, keepdims=True)  19.4 us
  transfers between devices with their start and end apart: 21, of which 21 were waited for; matrix products, arithmetic and copies ran while one was open for 2% of the time, Pallas kernels for 0%

commit v1 on v0

v1 whole, which is shorter than its diff:
```python
import functools
import math

import jax
import jax.numpy as jnp
from jax import lax
from jax.experimental import pallas as pl
from jax.experimental.pallas import tpu as pltpu
from jax.sharding import PartitionSpec as P

MESH = pl.DeviceIdType.MESH
CH = 512


def alibi_slopes(heads_n):
    closest = 2 ** int(math.floor(math.log2(heads_n)))
    base_rate = 2.0 ** (-8.0 / closest)
    slope_list = [base_rate ** (head_idx + 1) for head_idx in range(closest)]
    extra_rate = 2.0 ** (-4.0 / closest)
    slope_list = slope_list + [extra_rate ** (2 * head_idx + 1) for head_idx in range(min(closest, heads_n - closest))]
    return jnp.array(slope_list, dtype=jnp.float32)


def kernel(stages, micro_n, seq_n, model_n, hid_loc, heads_loc, head_dim,
           lens_ref, slopes_ref, x_hbm, wqkv_hbm, wout_hbm, wup_hbm, wdown_hbm,
           g1_ref, s1_ref, bqkv_ref, bo_ref, g2_ref, s2_ref, bup_ref, bd_ref,
           out_hbm,
           wqkv, wout, wup, wdown, xbuf, in1, in2, part, a_ref, u_ref, qkv, ctx, ctxb,
           wq_sem, wo_sem, wu_sem, wd_sem, x_sem, in1_sem, in2_sem, s1_sem, s2_sem, f_sem, o_sem):
    tp = lax.axis_index('tp')
    pp = lax.axis_index('pp')
    nc = model_n // CH
    nu = hid_loc // CH
    inner = (tp == 1) | (tp == 2)
    outer = (tp == 0) | (tp == 3)
    partner = tp + 1 - 2 * (tp % 2)
    peer = 3 - tp
    first = pp == 0
    later = pp > 0
    sends = pp < stages - 1

    def x_copy(u, c):
        return pltpu.make_async_copy(x_hbm.at[u, :, pl.ds(c * CH, CH)], xbuf.at[u, c], x_sem.at[u, c])

    def wq_copy(c):
        return pltpu.make_async_copy(wqkv_hbm.at[c], wqkv.at[c], wq_sem.at[c])

    def wo_copy(c):
        return pltpu.make_async_copy(wout_hbm.at[:, pl.ds(c * CH, CH)], wout.at[c], wo_sem.at[c])

    def wu_copy(c):
        return pltpu.make_async_copy(wup_hbm.at[:, pl.ds(c * CH, CH)], wup.at[c], wu_sem.at[c])

    def wd_copy(c):
        return pltpu.make_async_copy(wdown_hbm.at[:, pl.ds(c * CH, CH)], wdown.at[c], wd_sem.at[c])

    @pl.when(first)
    def _():
        for c in range(nc):
            x_copy(0, c).start()
    for c in range(3):
        wq_copy(c).start()
    for c in range(nc):
        wo_copy(c).start()
    for c in range(nu):
        wu_copy(c).start()
    for c in range(nc):
        wd_copy(c).start()

    @pl.when(first)
    def _():
        for u in range(1, micro_n):
            for c in range(nc):
                x_copy(u, c).start()

    barrier = pltpu.get_barrier_semaphore()
    links = ((tp > 0, {'tp': tp - 1}), (tp < 3, {'tp': tp + 1}), (later, {'pp': pp - 1}), (sends, {'pp': pp + 1}))
    for cond, dev in links:
        @pl.when(cond)
        def _(dev=dev):
            pl.semaphore_signal(barrier, inc=1, device_id=dev, device_id_type=MESH)
    pl.semaphore_wait(barrier, sum(cond.astype(jnp.int32) for cond, _ in links))

    def part_copy(k, c):
        return pltpu.make_async_remote_copy(
            src_ref=part.at[k % 2, c], dst_ref=in1.at[k, c], send_sem=s1_sem.at[k, c], recv_sem=in1_sem.at[k, c],
            device_id={'tp': partner}, device_id_type=MESH)

    def sum_copy(k, c):
        return pltpu.make_async_remote_copy(
            src_ref=part.at[k % 2, c], dst_ref=in2.at[k, c], send_sem=s1_sem.at[k, c], recv_sem=in2_sem.at[k, c],
            device_id={'tp': peer}, device_id_type=MESH)

    def res_copy(k, c):
        return pltpu.make_async_remote_copy(
            src_ref=in1.at[k, c], dst_ref=in1.at[k, c], send_sem=s2_sem.at[k, c], recv_sem=in1_sem.at[k, c],
            device_id={'tp': partner}, device_id_type=MESH)

    def fwd_copy(u, c):
        return pltpu.make_async_remote_copy(
            src_ref=in1.at[2 * u + 1, c], dst_ref=xbuf.at[u, c], send_sem=f_sem.at[u, c], recv_sem=x_sem.at[u, c],
            device_id={'pp': pp + 1}, device_id_type=MESH)

    def out_copy(u, c):
        return pltpu.make_async_copy(in1.at[2 * u + 1, c], out_hbm.at[u, :, pl.ds(c * CH, CH)], o_sem.at[u, c])

    def cols(c, width=CH):
        return pl.ds(pl.multiple_of(c * width, width), width)

    rows_blk = 32

    def layer_norm(src, idx, gain, shift):
        @pl.loop(0, seq_n // rows_blk)
        def _(r):
            rows = pl.ds(pl.multiple_of(r * rows_blk, rows_blk), rows_blk)
            val = jnp.concatenate([src[idx, c, rows, :] for c in range(nc)], axis=-1).astype(jnp.float32)
            mean = jnp.sum(val, axis=-1, keepdims=True) * (1.0 / model_n)
            cen = val - mean
            var = jnp.sum(cen * cen, axis=-1, keepdims=True) * (1.0 / model_n)
            normed = cen * lax.rsqrt(var + 1e-5)
            a_ref[rows, :] = (normed * gain[...].astype(jnp.float32) + shift[...].astype(jnp.float32)).astype(jnp.bfloat16)

    def attention(u):
        seq_len = lens_ref[u]
        qpos = lax.broadcasted_iota(jnp.int32, (seq_n, seq_n), 0)
        kpos = lax.broadcasted_iota(jnp.int32, (seq_n, seq_n), 1)
        allowed = (kpos <= qpos) & (kpos < seq_len)
        dist = (qpos - kpos).astype(jnp.float32)
        ctx[...] = jnp.zeros_like(ctx)

        @pl.loop(0, heads_loc // 2)
        def _(g):
            win = pl.ds(pl.multiple_of(g * 128, 128), 256)
            lane = lax.broadcasted_iota(jnp.int32, (1, 256), 1) + g * 128
            low = 2 * head_dim * g
            m0 = ((lane >= low) & (lane < low + head_dim)).astype(jnp.float32).astype(jnp.bfloat16)
            m1 = ((lane >= low + head_dim) & (lane < low + 2 * head_dim)).astype(jnp.float32).astype(jnp.bfloat16)
            key = qkv[1, :, win]
            val = qkv[2, :, win]
            kk = jnp.concatenate([key * m0, key * m1], axis=0)
            vv = jnp.concatenate([val * m0, val * m1], axis=0)
            sc = lax.dot_general(qkv[0, :, win], kk, (((1,), (1,)), ((), ())), preferred_element_type=jnp.float32)
            probs = []
            for j in range(2):
                s = sc[:, j * seq_n:(j + 1) * seq_n] * (head_dim ** -0.5)
                s = s - slopes_ref[tp * heads_loc + 2 * g + j] * dist
                s = jnp.where(allowed, s, -1e30)
                e = jnp.exp(s - jnp.max(s, axis=-1, keepdims=True))
                probs.append((e / jnp.sum(e, axis=-1, keepdims=True)).astype(jnp.bfloat16))
            o = jnp.dot(jnp.concatenate(probs, axis=-1), vv, preferred_element_type=jnp.float32)
            ctx[:, win] += o
        ctxb[...] = ctx[...].astype(jnp.bfloat16)

    def own_partial(s, a, lhs, w, w_copy):
        k = 2 * s + a

        @pl.loop(0, nc)
        def _(c):
            @pl.when(s == 0)
            def _():
                w_copy(c).wait()

            @pl.when(s > 0)
            def _():
                part_copy(k - 2, c).wait_send()
            part[a, c] = jnp.dot(lhs[...], w[c], preferred_element_type=jnp.float32).astype(jnp.bfloat16)

            @pl.when(outer)
            def _():
                part_copy(k, c).start()

    def p1(s):
        for c in range(nc):
            x_copy(s, c).wait()
        layer_norm(xbuf, s, g1_ref, s1_ref)

        for c in range(3):
            @pl.when(s == 0)
            def _(c=c):
                wq_copy(c).wait()
            acc = jnp.dot(a_ref[...], wqkv[c], preferred_element_type=jnp.float32)
            qkv[c] = (acc + bqkv_ref[c:c + 1, :].astype(jnp.float32)).astype(jnp.bfloat16)
        attention(s)
        own_partial(s, 0, ctxb, wout, wo_copy)

    def p2(s):
        layer_norm(in1, 2 * s, g2_ref, s2_ref)

        @pl.loop(0, nu)
        def _(c):
            @pl.when(s == 0)
            def _():
                wu_copy(c).wait()
            t = jnp.dot(a_ref[...], wup[c], preferred_element_type=jnp.float32) + bup_ref[:, cols(c)].astype(jnp.float32)
            t = 0.5 * t * (1.0 + jnp.tanh(math.sqrt(2.0 / math.pi) * (t + 0.044715 * (t * t * t))))
            u_ref[:, cols(c)] = t.astype(jnp.bfloat16)
        own_partial(s, 1, u_ref, wdown, wd_copy)

    def r1(s, a):
        k = 2 * s + a

        @pl.when(inner)
        def _():
            @pl.loop(0, nc)
            def _(c):
                part_copy(k, c).wait_recv()
                part[a, c] = (part[a, c].astype(jnp.float32) + in1[k, c].astype(jnp.float32)).astype(jnp.bfloat16)
                sum_copy(k, c).start()

    def r2(s, a):
        k = 2 * s + a
        bias = bo_ref if a == 0 else bd_ref

        @pl.loop(0, nc)
        def _(c):
            @pl.when(inner)
            def _():
                sum_copy(k, c).wait_recv()
                resid = xbuf[s, c] if a == 0 else in1[2 * s, c]
                total = part[a, c].astype(jnp.float32) + in2[k, c].astype(jnp.float32)
                in1[k, c] = (resid.astype(jnp.float32) + total + bias[:, cols(c)].astype(jnp.float32)).astype(jnp.bfloat16)
                res_copy(k, c).start()

            @pl.when(outer)
            def _():
                part_copy(k, c).wait_recv()
            if a == 1:
                @pl.when(sends)
                def _():
                    fwd_copy(s, c).start()
                out_copy(s, c).start()

    @pl.loop(0, micro_n + 1)
    def _(s):
        @pl.when(s > 0)
        def _():
            r1(s - 1, 1)

        @pl.when(s < micro_n)
        def _():
            p1(s)

        @pl.when(s > 0)
        def _():
            r2(s - 1, 1)

        @pl.when(s < micro_n)
        def _():
            r1(s, 0)
            r2(s, 0)
            p2(s)

    last = micro_n - 1
    for a in range(2):
        for c in range(nc):
            part_copy(2 * last + a, c).wait_send()

    @pl.when(inner)
    def _():
        @pl.loop(0, 2 * micro_n)
        def _(k):
            @pl.loop(0, nc)
            def _(c):
                res_copy(k, c).wait_send()

    @pl.loop(0, micro_n)
    def _(u):
        @pl.loop(0, nc)
        def _(c):
            @pl.when(sends)
            def _():
                fwd_copy(u, c).wait_send()
            out_copy(u, c).wait()


def solution(mesh):
    stages = mesh.shape['pp']
    in_specs = (P('dp'), P('dp'), P('pp'), P('pp'), P('pp', None, None, 'tp'), P('pp', None, 'tp', None), P('pp', 'tp', None), P('pp'), P('pp'), P('pp'), P('pp', None, 'tp'), P('pp', 'tp'), P('pp', 'tp', None), P('pp'))

    def per_device(x_in, seq_lens, ln1_gain, ln1_shift, w_qkv, b_qkv, w_out, b_out, ln2_gain, ln2_shift, w_up, b_up, w_down, b_down):
        micro_n, batch_n, seq_n, model_n = x_in.shape
        heads_loc, head_dim = b_qkv.shape[2], b_qkv.shape[3]
        width_loc = heads_loc * head_dim
        hid_loc = w_up.shape[2]
        nc, nu = model_n // CH, hid_loc // CH
        assert batch_n == 1 and mesh.shape['tp'] == 4 and seq_n == 128
        slopes = alibi_slopes(heads_loc * mesh.shape['tp'])
        bf = jnp.bfloat16
        vm = pl.BlockSpec(memory_space=pltpu.VMEM)
        sm = pl.BlockSpec(memory_space=pltpu.SMEM)
        hb = pl.BlockSpec(memory_space=pl.ANY)
        dma = pltpu.SemaphoreType.DMA
        body = functools.partial(kernel, stages, micro_n, seq_n, model_n, hid_loc, heads_loc, head_dim)
        out = pl.pallas_call(
            body,
            out_shape=jax.ShapeDtypeStruct((micro_n, seq_n, model_n), bf),
            in_specs=[sm, sm] + [hb] * 5 + [vm] * 8,
            out_specs=hb,
            scratch_shapes=[
                pltpu.VMEM((3, model_n, width_loc), bf),
                pltpu.VMEM((nc, width_loc, CH), bf),
                pltpu.VMEM((nu, model_n, CH), bf),
                pltpu.VMEM((nc, hid_loc, CH), bf),
                pltpu.VMEM((micro_n, nc, seq_n, CH), bf),
                pltpu.VMEM((2 * micro_n, nc, seq_n, CH), bf),
                pltpu.VMEM((2 * micro_n, nc, seq_n, CH), bf),
                pltpu.VMEM((2, nc, seq_n, CH), bf),
                pltpu.VMEM((seq_n, model_n), bf),
                pltpu.VMEM((seq_n, hid_loc), bf),
                pltpu.VMEM((3, seq_n, width_loc), bf),
                pltpu.VMEM((seq_n, width_loc), jnp.float32),
                pltpu.VMEM((seq_n, width_loc), bf),
                dma((3,)), dma((nc,)), dma((nu,)), dma((nc,)),
                dma((micro_n, nc)), dma((2 * micro_n, nc)), dma((2 * micro_n, nc)),
                dma((2 * micro_n, nc)), dma((2 * micro_n, nc)), dma((micro_n, nc)), dma((micro_n, nc)),
            ],
            compiler_params=pltpu.CompilerParams(
                collective_id=0, has_side_effects=True, vmem_limit_bytes=67043328),
            name='stages',
        )(
            seq_lens.reshape(micro_n), slopes,
            x_in.reshape(micro_n, seq_n, model_n),
            jnp.transpose(w_qkv[0], (1, 0, 2)), w_out[0], w_up[0], w_down[0],
            ln1_gain, ln1_shift, b_qkv.reshape(3, width_loc), b_out, ln2_gain, ln2_shift, b_up, b_down,
        )
        return out.reshape(1, micro_n, batch_n, seq_n, model_n)

    return jax.shard_map(per_device, mesh=mesh, in_specs=in_specs, out_specs=P('pp', 'dp'), check_vma=False)
```

time: 903 us -> 356 us (0.39); the launches traced: 893 us -> 356 us
  waiting for transfers between devices: 617 us -> 0 us
  Pallas kernels: 0 us -> 351 us
  matrix products: 174 us -> 0 us
  other arithmetic: 46.6 us -> 0 us
  local copies, waits for them, and re-layouts: 31 us -> 4.77 us
  between operations: 13.2 us -> 0.01 us
  starting transfers between devices: 9.39 us -> 0 us
    psum x14 -> x0, waiting for transfers between devices: 602 us -> none  [the longest x7 327 us: stage_layer(): attn_sum = lax.psum(attn_part.reshape(tokens_n, model_n), 'tp')]
    pallas_call x0 -> x1, Pallas kernels: none -> 351 us  [per_device(): pl.pallas_call(body, out_shape=jax.ShapeDtypeStruct((micro_n, seq_n, mode...]
    dot_general x28 -> x0, matrix products: 171 us -> none  [the longest x7 93.4 us: stage_layer(): jnp.dot(hidden_act, w_down, preferred_element_type=jnp.float32)]
    reduce_sum x28 -> x0, other arithmetic: 24 us -> none  [the longest x14 19.4 us: layer_norm(): mean_val = jnp.mean(val_f, axis=-1, keepdims=True)]
    ppermute x7 -> x0, waiting for transfers between devices: 15.5 us -> none  [one_step(): received = lax.ppermute(act_out, 'pp', next_pairs)]
    while x15 -> x0, local copies, waits for them, and re-layouts: 13.9 us -> none  [the longest x1 13.8 us: per_device(): lax.fori_loop(0, micro_n + stages - 1, one_step, loop_init)]
    dynamic_slice x15 -> x0, local copies, waits for them, and re-layouts: 12.8 us -> none  [the longest x7 7.95 us: one_step(): previous = lax.dynamic_index_in_dim(outputs, micro_idx, 0, keepdims=False)]
    reshape x7 -> x0, other arithmetic: 9.46 us -> none  [stage_layer(): return result.reshape(batch_n, seq_n, model_n)]
  transfers between devices with their start and end apart: 21 -> 0, of which waited for: 21 -> 0; matrix products, arithmetic and copies ran while one was open for 2% -> 0% of each run, Pallas kernels for 0% -> 0%
where the time goes in v1:
time: 356 us
  Pallas kernels  351 us (99%)
  local copies, waits for them, and re-layouts  4.77 us (1%)
    pallas_call x1, Pallas kernels, per_device(): pl.pallas_call(body, out_shape=jax.ShapeDtypeStruct((micro_n, seq_n, mode...  351 us

profile of v1, /device:TPU:5, one launch (start us, length us, event | category | flops | bytes accessed | tf_op | source)
XLA Modules:
  0.0 356.1 jit_solution(7208167392367392922)
XLA Ops:
  0.0 1.4 reshape.14.bqkv_ref
  1.4 351.3 %stages.1 = bf16[4,128,2560]{2,1,0:T(8,128)(2,1)} custom-call(s32[4]{0:T(128)} %bitcast.19, f32[32]{0:T(128)} %constant.2.clone.slopes_ref, bf16[4,128,2560]{2,1,0:T(8,128)(2,1)} %bitcast.18, bf16[3,2560,640]{2,1,0:T(8,128)(2,1)} %bitcast.16, bf16[640,2560]{1,0:T(8,128)(2,1)} %bitcast.17, bf16[2560,2560]{1,0:T(8,128)(2,1)} %bitcast.13, ...), custom_call_target="tpu_custom_call" | custom-call | tf_op jit(solution)/shard_map/stages/pallas_call | solution.py:294
  352.7 3.4 copy.18

commit v2 on v1

--- a/solution.py
+++ b/solution.py
@@ -9,7 +9,8 @@
 from jax.sharding import PartitionSpec as P
 
 MESH = pl.DeviceIdType.MESH
-CH = 512
+CH = 256
+WC = 512
 
 
 def alibi_slopes(heads_n):
@@ -30,7 +31,9 @@
     tp = lax.axis_index('tp')
     pp = lax.axis_index('pp')
     nc = model_n // CH
-    nu = hid_loc // CH
+    nw = model_n // WC
+    nu = hid_loc // WC
+    sub = WC // CH
     inner = (tp == 1) | (tp == 2)
     outer = (tp == 0) | (tp == 3)
     partner = tp + 1 - 2 * (tp % 2)
@@ -46,13 +49,13 @@
         return pltpu.make_async_copy(wqkv_hbm.at[c], wqkv.at[c], wq_sem.at[c])
 
     def wo_copy(c):
-        return pltpu.make_async_copy(wout_hbm.at[:, pl.ds(c * CH, CH)], wout.at[c], wo_sem.at[c])
+        return pltpu.make_async_copy(wout_hbm.at[:, pl.ds(c * WC, WC)], wout.at[c], wo_sem.at[c])
 
     def wu_copy(c):
-        return pltpu.make_async_copy(wup_hbm.at[:, pl.ds(c * CH, CH)], wup.at[c], wu_sem.at[c])
+        return pltpu.make_async_copy(wup_hbm.at[:, pl.ds(c * WC, WC)], wup.at[c], wu_sem.at[c])
 
     def wd_copy(c):
-        return pltpu.make_async_copy(wdown_hbm.at[:, pl.ds(c * CH, CH)], wdown.at[c], wd_sem.at[c])
+        return pltpu.make_async_copy(wdown_hbm.at[:, pl.ds(c * WC, WC)], wdown.at[c], wd_sem.at[c])
 
     @pl.when(first)
     def _():
@@ -60,11 +63,11 @@
             x_copy(0, c).start()
     for c in range(3):
         wq_copy(c).start()
-    for c in range(nc):
+    for c in range(nw):
         wo_copy(c).start()
     for c in range(nu):
         wu_copy(c).start()
-    for c in range(nc):
+    for c in range(nw):
         wd_copy(c).start()
 
     @pl.when(first)
@@ -154,20 +157,24 @@
     def own_partial(s, a, lhs, w, w_copy):
         k = 2 * s + a
 
-        @pl.loop(0, nc)
-        def _(c):
+        @pl.loop(0, nw)
+        def _(w_idx):
             @pl.when(s == 0)
             def _():
-                w_copy(c).wait()
+                w_copy(w_idx).wait()
 
             @pl.when(s > 0)
             def _():
-                part_copy(k - 2, c).wait_send()
-            part[a, c] = jnp.dot(lhs[...], w[c], preferred_element_type=jnp.float32).astype(jnp.bfloat16)
+                for j in range(sub):
+                    part_copy(k - 2, w_idx * sub + j).wait_send()
+            val = jnp.dot(lhs[...], w[w_idx], preferred_element_type=jnp.float32).astype(jnp.bfloat16)
+            for j in range(sub):
+                part[a, w_idx * sub + j] = val[:, j * CH:(j + 1) * CH]
 
             @pl.when(outer)
             def _():
-                part_copy(k, c).start()
+                for j in range(sub):
+                    part_copy(k, w_idx * sub + j).start()
 
     def p1(s):
         for c in range(nc):
@@ -191,9 +198,9 @@
             @pl.when(s == 0)
             def _():
                 wu_copy(c).wait()
-            t = jnp.dot(a_ref[...], wup[c], preferred_element_type=jnp.float32) + bup_ref[:, cols(c)].astype(jnp.float32)
+            t = jnp.dot(a_ref[...], wup[c], preferred_element_type=jnp.float32) + bup_ref[:, cols(c, WC)].astype(jnp.float32)
             t = 0.5 * t * (1.0 + jnp.tanh(math.sqrt(2.0 / math.pi) * (t + 0.044715 * (t * t * t))))
-            u_ref[:, cols(c)] = t.astype(jnp.bfloat16)
+            u_ref[:, cols(c, WC)] = t.astype(jnp.bfloat16)
         own_partial(s, 1, u_ref, wdown, wd_copy)
 
     def r1(s, a):
@@ -232,16 +239,13 @@
 
     @pl.loop(0, micro_n + 1)
     def _(s):
+        @pl.when(s < micro_n)
+        def _():
+            p1(s)
+
         @pl.when(s > 0)
         def _():
             r1(s - 1, 1)
-
-        @pl.when(s < micro_n)
-        def _():
-            p1(s)
-
-        @pl.when(s > 0)
-        def _():
             r2(s - 1, 1)
 
         @pl.when(s < micro_n)
@@ -282,7 +286,7 @@
         heads_loc, head_dim = b_qkv.shape[2], b_qkv.shape[3]
         width_loc = heads_loc * head_dim
         hid_loc = w_up.shape[2]
-        nc, nu = model_n // CH, hid_loc // CH
+        nc, nw, nu = model_n // CH, model_n // WC, hid_loc // WC
         assert batch_n == 1 and mesh.shape['tp'] == 4 and seq_n == 128
         slopes = alibi_slopes(heads_loc * mesh.shape['tp'])
         bf = jnp.bfloat16
@@ -298,9 +302,9 @@
             out_specs=hb,
             scratch_shapes=[
                 pltpu.VMEM((3, model_n, width_loc), bf),
-                pltpu.VMEM((nc, width_loc, CH), bf),
-                pltpu.VMEM((nu, model_n, CH), bf),
-                pltpu.VMEM((nc, hid_loc, CH), bf),
+                pltpu.VMEM((nw, width_loc, WC), bf),
+                pltpu.VMEM((nu, model_n, WC), bf),
+                pltpu.VMEM((nw, hid_loc, WC), bf),
                 pltpu.VMEM((micro_n, nc, seq_n, CH), bf),
                 pltpu.VMEM((2 * micro_n, nc, seq_n, CH), bf),
                 pltpu.VMEM((2 * micro_n, nc, seq_n, CH), bf),
@@ -310,7 +314,7 @@
                 pltpu.VMEM((3, seq_n, width_loc), bf),
                 pltpu.VMEM((seq_n, width_loc), jnp.float32),
                 pltpu.VMEM((seq_n, width_loc), bf),
-                dma((3,)), dma((nc,)), dma((nu,)), dma((nc,)),
+                dma((3,)), dma((nw,)), dma((nu,)), dma((nw,)),
                 dma((micro_n, nc)), dma((2 * micro_n, nc)), dma((2 * micro_n, nc)),
                 dma((2 * micro_n, nc)), dma((2 * micro_n, nc)), dma((micro_n, nc)), dma((micro_n, nc)),
             ],

time: 356 us -> 319 us (0.90)
  Pallas kernels: 351 us -> 313 us
    pallas_call x1, Pallas kernels: 351 us -> 313 us  [per_device(): pl.pallas_call(body, out_shape=jax.ShapeDtypeStruct((micro_n, seq_n, mode...]
where the time goes in v2:
time: 319 us; the launch traced here: 318 us
  Pallas kernels  313 us (98%)
  local copies, waits for them, and re-layouts  4.77 us (1%)
    pallas_call x1, Pallas kernels, per_device(): pl.pallas_call(body, out_shape=jax.ShapeDtypeStruct((micro_n, seq_n, mode...  313 us

profile of v2, /device:TPU:5, one launch (start us, length us, event | category | flops | bytes accessed | tf_op | source)
XLA Modules:
  0.0 318.2 jit_solution(16430639609405265115)
XLA Ops:
  0.0 1.4 reshape.14.bqkv_ref
  1.4 313.4 %stages.1 = bf16[4,128,2560]{2,1,0:T(8,128)(2,1)} custom-call(s32[4]{0:T(128)} %bitcast.19, f32[32]{0:T(128)} %constant.2.clone.slopes_ref, bf16[4,128,2560]{2,1,0:T(8,128)(2,1)} %bitcast.18, bf16[3,2560,640]{2,1,0:T(8,128)(2,1)} %bitcast.16, bf16[640,2560]{1,0:T(8,128)(2,1)} %bitcast.17, bf16[2560,2560]{1,0:T(8,128)(2,1)} %bitcast.13, ...), custom_call_target="tpu_custom_call" | custom-call | tf_op jit(solution)/shard_map/stages/pallas_call | solution.py:298
  314.8 3.4 %copy.18 = bf16[1,4,1,128,2560]{4,3,2,1,0:T(8,128)(2,1)} copy(bf16[1,4,1,128,2560]{4,3,2,1,0:T(8,128)(2,1)} %bitcast.15) | data formatting | bytes 5242880

commit v3 on v2

v3 whole, which is shorter than its diff:
```python
import functools
import math

import jax
import jax.numpy as jnp
from jax import lax
from jax.experimental import pallas as pl
from jax.experimental.pallas import tpu as pltpu
from jax.sharding import PartitionSpec as P

MESH = pl.DeviceIdType.MESH
CH = 512
WC = 512


def alibi_slopes(heads_n):
    closest = 2 ** int(math.floor(math.log2(heads_n)))
    base_rate = 2.0 ** (-8.0 / closest)
    slope_list = [base_rate ** (head_idx + 1) for head_idx in range(closest)]
    extra_rate = 2.0 ** (-4.0 / closest)
    slope_list = slope_list + [extra_rate ** (2 * head_idx + 1) for head_idx in range(min(closest, heads_n - closest))]
    return jnp.array(slope_list, dtype=jnp.float32)


TOK = 64
TABLES = {
    (0, 0): (
        2048, 18440, 34832, 274438, 798982, 4614, 28675, 553102, 1077646, 45066, 569494, 831499, 37398, 14355,
        538759, 1063303, 51224, 292879, 817423, 66063, 67607, 571543, 1096087, 84008, 323614, 848158, 53790, 55334,
        602278, 1126822, 94242, 356387, 880942, 86574, 88095, 587935, 1112479, 79920, 342065, 866599, 115239, 116783,
        620719, 1145263, 372790, 897334, 102966, 127027, 651454, 1175998, 120890, 374839, 899383, 129591, 653503, 1178047,
        3934080, 3934080, 3934080, 3934080, 3934080, 3934080, 3934080, 3934080, 3934080, 3934080, 3934080, 3934080, 3934080, 3934080,
        3934080, 3934080, 3934080, 3934080, 3934080, 3934080, 3934080, 3934080, 3934080, 3934080, 3934080, 3934080, 3934080, 3934080,
        3934080, 3934080, 3934080, 3934080, 3934080, 3934080, 3934080, 3934080, 3934080, 3934080, 3934080, 3934080,
    ),
    (0, 1): (
        2048, 18440, 8208, 532612, 35204, 25092, 549004, 811014, 1073286, 41222, 303494, 565766, 28674, 553102,
        1077646, 307222, 569748, 6676, 831498, 10774, 272395, 796933, 37381, 38919, 538759, 27015, 289287, 813325,
        49677, 30741, 567445, 829583, 1091855, 51599, 47631, 309280, 833815, 68119, 319516, 581672, 84380, 1105950,
        73886, 336158, 598430, 53790, 860198, 1122470, 55340, 352550, 864556, 877094, 94242, 1138862, 618531, 321565,
        584110, 86574, 845855, 326173, 587819, 337957, 850213, 1112485, 79920, 1124519, 100397, 354599, 866605, 1128877,
        96312, 358957, 620601, 368692, 631215, 893487, 1155126, 635062, 897084, 1159356, 647218, 127420, 389171, 651836,
        1175998, 108602, 121013, 895285, 113205, 637111, 1161655, 387133, 129341, 1173949, 653503, 1178047,
    ),
    (1, 0): (
        2048, 18440, 34832, 274438, 798982, 4614, 28675, 553102, 1077646, 22538, 307222, 831766, 1093639, 276498,
        538643, 1063303, 292879, 555032, 51599, 47631, 309280, 571425, 1096087, 61480, 323625, 848158, 53790, 55334,
        602278, 1126822, 94242, 356387, 880942, 86574, 63531, 587935, 98719, 80415, 342065, 866599, 96807, 620719,
        1145263, 110648, 116918, 897334, 102966, 127027, 651454, 1175998, 120890, 374839, 899383, 129591, 653503, 1178047,
        3934080, 3934080, 3934080, 3934080, 3934080, 3934080, 3934080, 3934080, 3934080, 3934080, 3934080, 3934080, 3934080, 3934080,
        3934080, 3934080, 3934080, 3934080, 3934080, 3934080, 3934080, 3934080, 3934080, 3934080, 3934080, 3934080, 3934080, 3934080,
        3934080, 3934080, 3934080, 3934080, 3934080, 3934080, 3934080, 3934080, 3934080, 3934080, 3934080, 3934080,
    ),
    (1, 1): (
        2048, 18440, 8208, 34948, 794884, 12804, 274444, 536716, 798988, 1061260, 28674, 1073294, 41230, 815252,
        565251, 1077652, 45066, 10390, 23060, 831766, 534661, 796679, 37398, 276997, 38925, 801031, 551053, 1063309,
        31245, 49295, 817423, 305173, 51727, 829717, 1091607, 309280, 67863, 57751, 320023, 82204, 323614, 1106332,
        585769, 335908, 598430, 1110436, 77850, 602278, 90660, 864428, 876844, 1126427, 70188, 356398, 880942, 59950,
        321571, 846109, 86557, 75807, 325675, 850207, 338463, 600103, 98725, 342565, 100397, 354599, 866605, 1141165,
        96807, 358452, 620724, 882996, 1145268, 110648, 635062, 1155510, 1159225, 104498, 385084, 909628, 127548, 651454,
        913461, 1175733, 119093, 374839, 637365, 121397, 1161655, 387133, 911677, 129597, 653503, 1178047,
    ),
    (2, 0): (
        2048, 18440, 274438, 536592, 35206, 4614, 28675, 553102, 1077646, 22538, 307222, 831766, 1093639, 38930,
        538759, 1063303, 292879, 49423, 51599, 66063, 47137, 571543, 833576, 84503, 323614, 848158, 53790, 77851,
        602278, 1126822, 71714, 356398, 880942, 1142832, 63537, 88106, 114847, 117023, 1112479, 342055, 866599, 111143,
        635062, 96694, 620719, 102966, 104879, 127535, 651454, 1175998, 120890, 374839, 899383, 129591, 653503, 1178047,
        3934080, 3934080, 3934080, 3934080, 3934080, 3934080, 3934080, 3934080, 3934080, 3934080, 3934080, 3934080, 3934080, 3934080,
        3934080, 3934080, 3934080, 3934080, 3934080, 3934080, 3934080, 3934080, 3934080, 3934080, 3934080, 3934080, 3934080, 3934080,
        3934080, 3934080, 3934080, 3934080, 3934080, 3934080, 3934080, 3934080, 3934080, 3934080, 3934080, 3934080,
    ),
    (2, 1): (
        2048, 18440, 270340, 794884, 12804, 32902, 798982, 25094, 286722, 811276, 6668, 34830, 553102, 41358,
        21006, 565396, 10644, 45588, 22661, 796933, 1058966, 831766, 1093639, 276498, 801031, 27143, 551053, 1075597,
        30739, 555151, 817176, 43535, 567445, 51605, 66069, 309271, 833815, 68119, 57384, 581788, 1106332, 61481,
        323620, 336158, 1110430, 53540, 860198, 90660, 352422, 55596, 876838, 864812, 70182, 356398, 59694, 72110,
        322094, 583722, 845855, 88605, 98463, 76063, 100517, 600479, 1112485, 115237, 342055, 368692, 893236, 92455,
        354727, 616999, 879156, 110649, 1140918, 123190, 96694, 358588, 620860, 102966, 909743, 1172015, 127027, 651454,
        1175998, 108602, 121013, 895285, 113205, 637111, 1161655, 387133, 911677, 1173567, 653503, 1178047,
    ),
    (3, 0): (
        2048, 18440, 274438, 798982, 4614, 6160, 28689, 553102, 1077646, 22538, 276487, 801031, 45575, 569494,
        1094038, 30738, 292883, 817423, 1079320, 65561, 47137, 571543, 61847, 1095720, 323625, 848158, 53790, 340006,
        55590, 1126822, 71714, 98350, 100526, 880942, 86574, 88095, 587935, 1112479, 114727, 604327, 117159, 111143,
        96438, 620719, 897334, 1159599, 127026, 105007, 651454, 1175998, 120890, 374839, 899383, 129591, 653503, 1178047,
        3934080, 3934080, 3934080, 3934080, 3934080, 3934080, 3934080, 3934080, 3934080, 3934080, 3934080, 3934080, 3934080, 3934080,
        3934080, 3934080, 3934080, 3934080, 3934080, 3934080, 3934080, 3934080, 3934080, 3934080, 3934080, 3934080, 3934080, 3934080,
        3934080, 3934080, 3934080, 3934080, 3934080, 3934080, 3934080, 3934080, 3934080, 3934080, 3934080, 3934080,
    ),
    (3, 1): (
        2048, 18440, 270340, 794884, 12804, 32902, 798982, 35334, 24578, 549004, 811011, 29196, 553102, 10638,
        21006, 534661, 1059205, 14356, 303115, 565383, 801031, 1063316, 45588, 307213, 569485, 831757, 1094029, 30738,
        1075343, 555027, 49551, 51727, 65557, 67733, 47381, 1091989, 57495, 571548, 844060, 1106327, 61480, 74263,
        323748, 860452, 84516, 848158, 53790, 340006, 864550, 55846, 90146, 614572, 1139116, 94243, 356400, 880942,
        321565, 584238, 86429, 64029, 337957, 862501, 1124511, 88351, 1112479, 100391, 604327, 106919, 92711, 368813,
        631085, 879028, 1141300, 114742, 96438, 620719, 117046, 883126, 1159228, 1145020, 127026, 909628, 1171646, 651315,
        1175998, 120890, 370741, 895285, 113205, 637111, 899133, 1161405, 911677, 129597, 653503, 1178047,
    ),
}


def kernel(stages, micro_n, seq_n, model_n, hid_loc, heads_loc, head_dim,
           lens_ref, slopes_ref, x_hbm, wqkv_hbm, wout_hbm, wup_hbm, wdown_hbm,
           g1_ref, s1_ref, bqkv_ref, bo_ref, g2_ref, s2_ref, bup_ref, bd_ref,
           out_hbm,
           wqkv, wout, wup, wdown, xbuf, in1, in2, part, a_ref, u_ref, q_ref, kv_ref, ctx, ctxb,
           wq_sem, wo_sem, wu_sem, wd_sem, x_sem, in1_sem, in2_sem, s1_sem, s2_sem, f_sem, o_sem):
    tp = lax.axis_index('tp')
    pp = lax.axis_index('pp')
    nc = model_n // CH
    nw = model_n // WC
    nu = hid_loc // WC
    sub = WC // CH
    halves = seq_n // TOK
    units = micro_n * halves
    inner = (tp == 1) | (tp == 2)
    outer = (tp == 0) | (tp == 3)
    partner = tp + 1 - 2 * (tp % 2)
    peer = 3 - tp
    first = pp == 0
    later = pp > 0
    sends = pp < stages - 1

    def where(u):
        return lax.div(u, halves), pl.ds(pl.multiple_of(lax.rem(u, halves) * TOK, TOK), TOK)

    def x_copy(u, c):
        m, rows = where(u)
        return pltpu.make_async_copy(x_hbm.at[m, rows, pl.ds(c * CH, CH)], xbuf.at[u, c], x_sem.at[u, c])

    def wq_copy(c):
        return pltpu.make_async_copy(wqkv_hbm.at[c], wqkv.at[c], wq_sem.at[c])

    def wo_copy(c):
        return pltpu.make_async_copy(wout_hbm.at[:, pl.ds(c * WC, WC)], wout.at[c], wo_sem.at[c])

    def wu_copy(c):
        return pltpu.make_async_copy(wup_hbm.at[:, pl.ds(c * WC, WC)], wup.at[c], wu_sem.at[c])

    def wd_copy(c):
        return pltpu.make_async_copy(wdown_hbm.at[:, pl.ds(c * WC, WC)], wdown.at[c], wd_sem.at[c])

    @pl.when(first)
    def _():
        for c in range(nc):
            x_copy(jnp.int32(0), c).start()
    for c in range(3):
        wq_copy(c).start()
    for c in range(nw):
        wo_copy(c).start()
    for c in range(nu):
        wu_copy(c).start()
    for c in range(nw):
        wd_copy(c).start()

    @pl.when(first)
    def _():
        @pl.loop(1, units)
        def _(u):
            for c in range(nc):
                x_copy(u, c).start()

    barrier = pltpu.get_barrier_semaphore()
    links = ((tp > 0, {'tp': tp - 1}), (tp < 3, {'tp': tp + 1}), (later, {'pp': pp - 1}), (sends, {'pp': pp + 1}))
    for cond, dev in links:
        @pl.when(cond)
        def _(dev=dev):
            pl.semaphore_signal(barrier, inc=1, device_id=dev, device_id_type=MESH)
    mine = [(((pp == stage) & (inner if role else outer)).astype(jnp.int32), words) for (stage, role), words in TABLES.items()]
    table = [sum(sel * words[j] for sel, words in mine) for j in range(len(TABLES[0, 0]))]
    pl.semaphore_wait(barrier, sum(cond.astype(jnp.int32) for cond, _ in links))

    def part_copy(k, c):
        return pltpu.make_async_remote_copy(
            src_ref=part.at[k, c], dst_ref=in1.at[k, c], send_sem=s1_sem.at[k, c], recv_sem=in1_sem.at[k, c],
            device_id={'tp': partner}, device_id_type=MESH)

    def sum_copy(k, c):
        return pltpu.make_async_remote_copy(
            src_ref=part.at[k, c], dst_ref=in2.at[k, c], send_sem=s1_sem.at[k, c], recv_sem=in2_sem.at[k, c],
            device_id={'tp': peer}, device_id_type=MESH)

    def res_copy(k, c):
        return pltpu.make_async_remote_copy(
            src_ref=in1.at[k, c], dst_ref=in1.at[k, c], send_sem=s2_sem.at[k, c], recv_sem=in1_sem.at[k, c],
            device_id={'tp': partner}, device_id_type=MESH)

    def fwd_copy(u, c):
        return pltpu.make_async_remote_copy(
            src_ref=in1.at[2 * u + 1, c], dst_ref=xbuf.at[u, c], send_sem=f_sem.at[u, c], recv_sem=x_sem.at[u, c],
            device_id={'pp': pp + 1}, device_id_type=MESH)

    def out_copy(u, c):
        m, rows = where(u)
        return pltpu.make_async_copy(
            in1.at[2 * u + 1, c], out_hbm.at[m, rows, pl.ds(pl.multiple_of(c * CH, CH), CH)], o_sem.at[u, c])

    def cols(c, width=CH):
        return pl.ds(pl.multiple_of(c * width, width), width)

    rows_blk = 32

    def layer_norm(src, idx, gain, shift):
        @pl.loop(0, TOK // rows_blk)
        def _(r):
            rows = pl.ds(pl.multiple_of(r * rows_blk, rows_blk), rows_blk)
            val = jnp.concatenate([src[idx, c, rows, :] for c in range(nc)], axis=-1).astype(jnp.float32)
            mean = jnp.sum(val, axis=-1, keepdims=True) * (1.0 / model_n)
            cen = val - mean
            var = jnp.sum(cen * cen, axis=-1, keepdims=True) * (1.0 / model_n)
            normed = cen * lax.rsqrt(var + 1e-5)
            a_ref[rows, :] = (normed * gain[...].astype(jnp.float32) + shift[...].astype(jnp.float32)).astype(jnp.bfloat16)

    def attention(u):
        m = lax.div(u, halves)
        seq_len = lens_ref[m]
        qpos = lax.broadcasted_iota(jnp.int32, (TOK, seq_n), 0) + lax.rem(u, halves) * TOK
        kpos = lax.broadcasted_iota(jnp.int32, (TOK, seq_n), 1)
        allowed = (kpos <= qpos) & (kpos < seq_len)
        dist = (qpos - kpos).astype(jnp.float32)
        ctx[...] = jnp.zeros_like(ctx)

        @pl.loop(0, heads_loc // 2)
        def _(g):
            win = pl.ds(pl.multiple_of(g * 128, 128), 256)
            lane = lax.broadcasted_iota(jnp.int32, (1, 256), 1) + g * 128
            low = 2 * head_dim * g
            m0 = ((lane >= low) & (lane < low + head_dim)).astype(jnp.float32).astype(jnp.bfloat16)
            m1 = ((lane >= low + head_dim) & (lane < low + 2 * head_dim)).astype(jnp.float32).astype(jnp.bfloat16)
            key = kv_ref[0, :, win]
            val = kv_ref[1, :, win]
            kk = jnp.concatenate([key * m0, key * m1], axis=0)
            vv = jnp.concatenate([val * m0, val * m1], axis=0)
            sc = lax.dot_general(q_ref[:, win], kk, (((1,), (1,)), ((), ())), preferred_element_type=jnp.float32)
            probs = []
            for j in range(2):
                s = sc[:, j * seq_n:(j + 1) * seq_n] * (head_dim ** -0.5)
                s = s - slopes_ref[tp * heads_loc + 2 * g + j] * dist
                s = jnp.where(allowed, s, -1e30)
                e = jnp.exp(s - jnp.max(s, axis=-1, keepdims=True))
                probs.append((e / jnp.sum(e, axis=-1, keepdims=True)).astype(jnp.bfloat16))
            o = jnp.dot(jnp.concatenate(probs, axis=-1), vv, preferred_element_type=jnp.float32)
            ctx[:, win] += o
        ctxb[...] = ctx[...].astype(jnp.bfloat16)

    def own_partial(u, a, lhs, w, w_copy):
        k = 2 * u + a

        @pl.loop(0, nw)
        def _(w_idx):
            @pl.when(u == 0)
            def _():
                w_copy(w_idx).wait()
            val = jnp.dot(lhs[...], w[w_idx], preferred_element_type=jnp.float32).astype(jnp.bfloat16)
            for j in range(sub):
                part[k, w_idx * sub + j] = val[:, j * CH:(j + 1) * CH]

            @pl.when(outer)
            def _():
                for j in range(sub):
                    part_copy(k, w_idx * sub + j).start()

    def p1a(u):
        _, rows = where(u)
        for c in range(nc):
            x_copy(u, c).wait()
        layer_norm(xbuf, u, g1_ref, s1_ref)
        if halves > 1:
            @pl.when(lax.rem(u, halves) == 0)
            def _():
                kv_ref[:, TOK:, :] = jnp.zeros((2, seq_n - TOK, kv_ref.shape[2]), kv_ref.dtype)
        for c in range(3):
            @pl.when(u == 0)
            def _(c=c):
                wq_copy(c).wait()
            acc = jnp.dot(a_ref[...], wqkv[c], preferred_element_type=jnp.float32)
            acc = (acc + bqkv_ref[c:c + 1, :].astype(jnp.float32)).astype(jnp.bfloat16)
            if c == 0:
                q_ref[...] = acc
            else:
                kv_ref[c - 1, rows, :] = acc

    def p1b(u):
        attention(u)
        own_partial(u, 0, ctxb, wout, wo_copy)

    def p2a(u):
        layer_norm(in1, 2 * u, g2_ref, s2_ref)

        @pl.loop(0, nu)
        def _(c):
            @pl.when(u == 0)
            def _():
                wu_copy(c).wait()
            t = jnp.dot(a_ref[...], wup[c], preferred_element_type=jnp.float32) + bup_ref[:, cols(c, WC)].astype(jnp.float32)
            t = 0.5 * t * (1.0 + jnp.tanh(math.sqrt(2.0 / math.pi) * (t + 0.044715 * (t * t * t))))
            u_ref[:, cols(c, WC)] = t.astype(jnp.bfloat16)

    def p2b(u):
        own_partial(u, 1, u_ref, wdown, wd_copy)

    def r1(u, a, c):
        k = 2 * u + a
        part_copy(k, c).wait_recv()
        part[k, c] = (part[k, c].astype(jnp.float32) + in1[k, c].astype(jnp.float32)).astype(jnp.bfloat16)
        sum_copy(k, c).start()

    def r2(u, a, c):
        k = 2 * u + a
        bias = bo_ref if a == 0 else bd_ref

        @pl.when(inner)
        def _():
            sum_copy(k, c).wait_recv()
            resid = xbuf[u, c] if a == 0 else in1[2 * u, c]
            total = part[k, c].astype(jnp.float32) + in2[k, c].astype(jnp.float32)
            in1[k, c] = (resid.astype(jnp.float32) + total + bias[:, cols(c)].astype(jnp.float32)).astype(jnp.bfloat16)
            res_copy(k, c).start()

        @pl.when(outer)
        def _():
            part_copy(k, c).wait_recv()
        if a == 1:
            @pl.when(sends)
            def _():
                fwd_copy(u, c).start()
            out_copy(u, c).start()

    ops = (p1a, p1b, p2a, p2b)

    def step(_, word):
        entry = lax.rem(word, 2048)
        op, u, c = lax.rem(entry, 8), lax.rem(lax.div(entry, 8), 16), lax.div(entry, 128)

        @pl.when(op < 4)
        def _():
            for i, fn in enumerate(ops):
                @pl.when((op == i) & (c == 0))
                def _(fn=fn):
                    fn(u)

        @pl.when(op >= 4)
        def _():
            for a in range(2):
                @pl.when(op == 4 + a)
                def _(a=a):
                    r1(u, a, c)

                @pl.when(op == 6 + a)
                def _(a=a):
                    r2(u, a, c)
        return lax.div(word, 2048)

    @pl.loop(0, len(TABLES[0, 0]))
    def _(t):
        lax.fori_loop(0, 2, step, sum((t == j).astype(jnp.int32) * word for j, word in enumerate(table)))

    @pl.loop(0, 2 * units)
    def _(k):
        for c in range(nc):
            part_copy(k, c).wait_send()

        @pl.when(inner)
        def _():
            for c in range(nc):
                res_copy(k, c).wait_send()

    @pl.loop(0, units)
    def _(u):
        @pl.when(sends)
        def _():
            for c in range(nc):
                fwd_copy(u, c).wait_send()
        for c in range(nc):
            out_copy(u, c).wait()


def solution(mesh):
    stages = mesh.shape['pp']
    in_specs = (P('dp'), P('dp'), P('pp'), P('pp'), P('pp', None, None, 'tp'), P('pp', None, 'tp', None), P('pp', 'tp', None), P('pp'), P('pp'), P('pp'), P('pp', None, 'tp'), P('pp', 'tp'), P('pp', 'tp', None), P('pp'))

    def per_device(x_in, seq_lens, ln1_gain, ln1_shift, w_qkv, b_qkv, w_out, b_out, ln2_gain, ln2_shift, w_up, b_up, w_down, b_down):
        micro_n, batch_n, seq_n, model_n = x_in.shape
        heads_loc, head_dim = b_qkv.shape[2], b_qkv.shape[3]
        width_loc = heads_loc * head_dim
        hid_loc = w_up.shape[2]
        nc, nw, nu = model_n // CH, model_n // WC, hid_loc // WC
        units = micro_n * seq_n // TOK
        assert batch_n == 1 and mesh.shape['tp'] == 4 and seq_n == 128
        slopes = alibi_slopes(heads_loc * mesh.shape['tp'])
        bf = jnp.bfloat16
        vm = pl.BlockSpec(memory_space=pltpu.VMEM)
        sm = pl.BlockSpec(memory_space=pltpu.SMEM)
        hb = pl.BlockSpec(memory_space=pl.ANY)
        dma = pltpu.SemaphoreType.DMA
        body = functools.partial(kernel, stages, micro_n, seq_n, model_n, hid_loc, heads_loc, head_dim)
        out = pl.pallas_call(
            body,
            out_shape=jax.ShapeDtypeStruct((micro_n, seq_n, model_n), bf),
            in_specs=[sm, sm] + [hb] * 5 + [vm] * 8,
            out_specs=hb,
            scratch_shapes=[
                pltpu.VMEM((3, model_n, width_loc), bf),
                pltpu.VMEM((nw, width_loc, WC), bf),
                pltpu.VMEM((nu, model_n, WC), bf),
                pltpu.VMEM((nw, hid_loc, WC), bf),
                pltpu.VMEM((units, nc, TOK, CH), bf),
                pltpu.VMEM((2 * units, nc, TOK, CH), bf),
                pltpu.VMEM((2 * units, nc, TOK, CH), bf),
                pltpu.VMEM((2 * units, nc, TOK, CH), bf),
                pltpu.VMEM((TOK, model_n), bf),
                pltpu.VMEM((TOK, hid_loc), bf),
                pltpu.VMEM((TOK, width_loc), bf),
                pltpu.VMEM((2, seq_n, width_loc), bf),
                pltpu.VMEM((TOK, width_loc), jnp.float32),
                pltpu.VMEM((TOK, width_loc), bf),
                dma((3,)), dma((nw,)), dma((nu,)), dma((nw,)),
                dma((units, nc)), dma((2 * units, nc)), dma((2 * units, nc)),
                dma((2 * units, nc)), dma((2 * units, nc)), dma((units, nc)), dma((units, nc)),
            ],
            compiler_params=pltpu.CompilerParams(
                collective_id=0, has_side_effects=True, vmem_limit_bytes=67043328),
            name='stages',
        )(
            seq_lens.reshape(micro_n), slopes,
            x_in.reshape(micro_n, seq_n, model_n),
            jnp.transpose(w_qkv[0], (1, 0, 2)), w_out[0], w_up[0], w_down[0],
            ln1_gain, ln1_shift, b_qkv.reshape(3, width_loc), b_out, ln2_gain, ln2_shift, b_up, b_down,
        )
        return out.reshape(1, micro_n, batch_n, seq_n, model_n)

    return jax.shard_map(per_device, mesh=mesh, in_specs=in_specs, out_specs=P('pp', 'dp'), check_vma=False)
```

time: 319 us -> 335 us (1.050)
  Pallas kernels: 313 us -> 330 us
    pallas_call x1, Pallas kernels: 313 us -> 330 us  [per_device(): pl.pallas_call(body, out_shape=jax.ShapeDtypeStruct((micro_n, seq_n, mode...]
where the time goes in v3:
time: 335 us
  Pallas kernels  330 us (99%)
  local copies, waits for them, and re-layouts  4.77 us (1%)
    pallas_call x1, Pallas kernels, per_device(): pl.pallas_call(body, out_shape=jax.ShapeDtypeStruct((micro_n, seq_n, mode...  330 us

profile of v3, /device:TPU:5, one launch (start us, length us, event | category | flops | bytes accessed | tf_op | source)
XLA Modules:
  0.0 334.8 jit_solution(2705950633045453447)
XLA Ops:
  0.0 1.4 reshape.14.bqkv_ref
  1.4 330.0 %stages.1 = bf16[4,128,2560]{2,1,0:T(8,128)(2,1)} custom-call(s32[4]{0:T(128)} %bitcast.19, f32[32]{0:T(128)} %constant.2.clone.slopes_ref, bf16[4,128,2560]{2,1,0:T(8,128)(2,1)} %bitcast.18, bf16[3,2560,640]{2,1,0:T(8,128)(2,1)} %bitcast.16, bf16[640,2560]{1,0:T(8,128)(2,1)} %bitcast.17, bf16[2560,2560]{1,0:T(8,128)(2,1)} %bitcast.13, ...), custom_call_target="tpu_custom_call" | custom-call | tf_op jit(solution)/shard_map/stages/pallas_call | solution.py:397
  331.4 3.4 %copy.18 = bf16[1,4,1,128,2560]{4,3,2,1,0:T(8,128)(2,1)} copy(bf16[1,4,1,128,2560]{4,3,2,1,0:T(8,128)(2,1)} %bitcast.15) | data formatting | bytes 5242880

commit v4 on v3

--- a/solution.py
+++ b/solution.py
@@ -25,76 +25,76 @@
 TOK = 64
 TABLES = {
     (0, 0): (
-        2048, 18440, 34832, 274438, 798982, 4614, 28675, 553102, 1077646, 45066, 569494, 831499, 37398, 14355,
-        538759, 1063303, 51224, 292879, 817423, 66063, 67607, 571543, 1096087, 84008, 323614, 848158, 53790, 55334,
-        602278, 1126822, 94242, 356387, 880942, 86574, 88095, 587935, 1112479, 79920, 342065, 866599, 115239, 116783,
-        620719, 1145263, 372790, 897334, 102966, 127027, 651454, 1175998, 120890, 374839, 899383, 129591, 653503, 1178047,
+        2048, 18440, 34832, 51224, 67616, 274438, 798982, 4614, 815246, 6158, 1077518, 45066, 22806, 1094038,
+        37014, 323614, 1110302, 847891, 55322, 276487, 801031, 82439, 30761, 555151, 1079695, 602160, 77990, 864305,
+        1126423, 309282, 571427, 1096087, 325688, 849977, 64031, 587822, 618670, 1143214, 110634, 372779, 897334, 102966,
+        104487, 604327, 1128871, 389182, 913726, 119358, 120879, 620719, 1145263, 374839, 899383, 129591, 653503, 1178047,
         3934080, 3934080, 3934080, 3934080, 3934080, 3934080, 3934080, 3934080, 3934080, 3934080, 3934080, 3934080, 3934080, 3934080,
         3934080, 3934080, 3934080, 3934080, 3934080, 3934080, 3934080, 3934080, 3934080, 3934080, 3934080, 3934080, 3934080, 3934080,
         3934080, 3934080, 3934080, 3934080, 3934080, 3934080, 3934080, 3934080, 3934080, 3934080, 3934080, 3934080,
     ),
     (0, 1): (
-        2048, 18440, 8208, 532612, 35204, 25092, 549004, 811014, 1073286, 41222, 303494, 565766, 28674, 553102,
-        1077646, 307222, 569748, 6676, 831498, 10774, 272395, 796933, 37381, 38919, 538759, 27015, 289287, 813325,
-        49677, 30741, 567445, 829583, 1091855, 51599, 47631, 309280, 833815, 68119, 319516, 581672, 84380, 1105950,
-        73886, 336158, 598430, 53790, 860198, 1122470, 55340, 352550, 864556, 877094, 94242, 1138862, 618531, 321565,
-        584110, 86574, 845855, 326173, 587819, 337957, 850213, 1112485, 79920, 1124519, 100397, 354599, 866605, 1128877,
-        96312, 358957, 620601, 368692, 631215, 893487, 1155126, 635062, 897084, 1159356, 647218, 127420, 389171, 651836,
-        1175998, 108602, 121013, 895285, 113205, 637111, 1161655, 387133, 129341, 1173949, 653503, 1178047,
+        2048, 18440, 8208, 34948, 794884, 1056792, 286732, 548870, 274457, 811270, 1073542, 65556, 29190, 303246,
+        553236, 1089940, 57742, 1077404, 45058, 307484, 831766, 844310, 61980, 323587, 20766, 272389, 534942, 23070,
+        1059205, 26657, 14477, 550948, 336007, 539021, 1075492, 860551, 1063460, 30738, 77967, 555027, 305173, 829717,
+        817685, 340495, 864550, 47130, 55846, 59543, 583837, 833815, 1108381, 70167, 63528, 71839, 84255, 850463,
+        352300, 876844, 98860, 106545, 630964, 1155508, 94245, 337976, 618670, 600121, 1143214, 862250, 111141, 372779,
+        634940, 897212, 1159484, 79922, 1171900, 342067, 1128743, 92583, 127149, 389421, 651693, 913965, 1175605, 118965,
+        96565, 895035, 1157295, 882991, 113199, 637111, 899133, 1161405, 911677, 1173567, 653503, 1178047,
     ),
     (1, 0): (
-        2048, 18440, 34832, 274438, 798982, 4614, 28675, 553102, 1077646, 22538, 307222, 831766, 1093639, 276498,
-        538643, 1063303, 292879, 555032, 51599, 47631, 309280, 571425, 1096087, 61480, 323625, 848158, 53790, 55334,
-        602278, 1126822, 94242, 356387, 880942, 86574, 63531, 587935, 98719, 80415, 342065, 866599, 96807, 620719,
-        1145263, 110648, 116918, 897334, 102966, 127027, 651454, 1175998, 120890, 374839, 899383, 129591, 653503, 1178047,
+        2048, 18440, 12304, 274449, 798982, 4614, 290830, 552963, 51224, 1077646, 45066, 307211, 831766, 37398,
+        14355, 538759, 1063303, 61472, 323617, 848158, 53790, 55311, 555151, 82319, 84495, 309271, 833815, 1095728,
+        340017, 78118, 1126822, 63522, 71839, 850207, 1112120, 356398, 618553, 1143214, 110634, 634923, 1159606, 102582,
+        342055, 604211, 1128871, 127023, 651454, 620719, 883134, 119358, 113199, 374843, 899383, 129591, 653503, 1178047,
         3934080, 3934080, 3934080, 3934080, 3934080, 3934080, 3934080, 3934080, 3934080, 3934080, 3934080, 3934080, 3934080, 3934080,
         3934080, 3934080, 3934080, 3934080, 3934080, 3934080, 3934080, 3934080, 3934080, 3934080, 3934080, 3934080, 3934080, 3934080,
         3934080, 3934080, 3934080, 3934080, 3934080, 3934080, 3934080, 3934080, 3934080, 3934080, 3934080, 3934080,
     ),
     (1, 1): (
-        2048, 18440, 8208, 34948, 794884, 12804, 274444, 536716, 798988, 1061260, 28674, 1073294, 41230, 815252,
-        565251, 1077652, 45066, 10390, 23060, 831766, 534661, 796679, 37398, 276997, 38925, 801031, 551053, 1063309,
-        31245, 49295, 817423, 305173, 51727, 829717, 1091607, 309280, 67863, 57751, 320023, 82204, 323614, 1106332,
-        585769, 335908, 598430, 1110436, 77850, 602278, 90660, 864428, 876844, 1126427, 70188, 356398, 880942, 59950,
-        321571, 846109, 86557, 75807, 325675, 850207, 338463, 600103, 98725, 342565, 100397, 354599, 866605, 1141165,
-        96807, 358452, 620724, 882996, 1145268, 110648, 635062, 1155510, 1159225, 104498, 385084, 909628, 127548, 651454,
-        913461, 1175733, 119093, 374839, 637365, 121397, 1161655, 387133, 911677, 129597, 653503, 1178047,
+        2048, 18440, 270340, 12304, 794884, 274449, 25092, 286982, 1061254, 4364, 290830, 1073548, 552963, 49172,
+        815252, 1077273, 20756, 827414, 307732, 569355, 272389, 831749, 1094021, 14354, 1058844, 319623, 538643, 844060,
+        1106311, 27143, 61472, 67725, 585886, 551309, 1075614, 53790, 305173, 55311, 829717, 293397, 73999, 336271,
+        1079588, 82340, 1122327, 83997, 309527, 833693, 584215, 845872, 78365, 100518, 90406, 614572, 876966, 1126956,
+        63522, 587935, 849955, 1112110, 356404, 114868, 880942, 631342, 892982, 373300, 86073, 337957, 635173, 897445,
+        1124918, 79915, 385084, 647335, 92210, 866599, 1128621, 127277, 909502, 651693, 1141308, 96307, 358453, 913711,
+        633013, 895407, 119358, 1145397, 374839, 121143, 1161655, 387133, 911677, 129597, 653503, 1178047,
     ),
     (2, 0): (
-        2048, 18440, 274438, 536592, 35206, 4614, 28675, 553102, 1077646, 22538, 307222, 831766, 1093639, 38930,
-        538759, 1063303, 292879, 49423, 51599, 66063, 47137, 571543, 833576, 84503, 323614, 848158, 53790, 77851,
-        602278, 1126822, 71714, 356398, 880942, 1142832, 63537, 88106, 114847, 117023, 1112479, 342055, 866599, 111143,
-        635062, 96694, 620719, 102966, 104879, 127535, 651454, 1175998, 120890, 374839, 899383, 129591, 653503, 1178047,
+        2048, 274438, 536584, 18822, 4614, 32771, 28689, 553102, 815128, 1077273, 20487, 538759, 800779, 45575,
+        569494, 1094038, 38930, 67616, 323614, 848158, 53790, 292879, 81947, 84367, 1079344, 47153, 309519, 833815,
+        78359, 114854, 864287, 117030, 587935, 1126815, 618530, 94751, 356387, 1143214, 88106, 897206, 110782, 635446,
+        127026, 651315, 80318, 119358, 342075, 604711, 96679, 620719, 1145263, 374839, 899383, 129591, 653503, 1178047,
         3934080, 3934080, 3934080, 3934080, 3934080, 3934080, 3934080, 3934080, 3934080, 3934080, 3934080, 3934080, 3934080, 3934080,
         3934080, 3934080, 3934080, 3934080, 3934080, 3934080, 3934080, 3934080, 3934080, 3934080, 3934080, 3934080, 3934080, 3934080,
         3934080, 3934080, 3934080, 3934080, 3934080, 3934080, 3934080, 3934080, 3934080, 3934080, 3934080, 3934080,
     ),
     (2, 1): (
-        2048, 18440, 270340, 794884, 12804, 32902, 798982, 25094, 286722, 811276, 6668, 34830, 553102, 41358,
-        21006, 565396, 10644, 45588, 22661, 796933, 1058966, 831766, 1093639, 276498, 801031, 27143, 551053, 1075597,
-        30739, 555151, 817176, 43535, 567445, 51605, 66069, 309271, 833815, 68119, 57384, 581788, 1106332, 61481,
-        323620, 336158, 1110430, 53540, 860198, 90660, 352422, 55596, 876838, 864812, 70182, 356398, 59694, 72110,
-        322094, 583722, 845855, 88605, 98463, 76063, 100517, 600479, 1112485, 115237, 342055, 368692, 893236, 92455,
-        354727, 616999, 879156, 110649, 1140918, 123190, 96694, 358588, 620860, 102966, 909743, 1172015, 127027, 651454,
-        1175998, 108602, 121013, 895285, 113205, 637111, 1161655, 387133, 911677, 1173567, 653503, 1178047,
+        2048, 270340, 794884, 16900, 274438, 18694, 1061254, 6146, 34832, 286732, 811276, 10764, 272398, 534670,
+        49422, 1059205, 815111, 277006, 303124, 565511, 51604, 21012, 1063303, 307222, 569355, 1094038, 57362, 39068,
+        844060, 66076, 288781, 61709, 323981, 585761, 848397, 53790, 292879, 55567, 305173, 82319, 829717, 1079829,
+        73769, 335895, 309540, 98724, 571421, 321943, 1096228, 78109, 845873, 340509, 864550, 90143, 325804, 114988,
+        850207, 877094, 1139231, 94260, 356386, 368942, 71988, 1143214, 1155508, 116790, 372778, 634940, 88252, 647606,
+        1159612, 75826, 1171518, 337971, 651454, 913701, 80293, 1176101, 92218, 342189, 121127, 866605, 1128877, 96813,
+        358453, 620725, 882997, 1145269, 113205, 374845, 637117, 899389, 1161661, 129597, 653503, 1178047,
     ),
     (3, 0): (
-        2048, 18440, 274438, 798982, 4614, 6160, 28689, 553102, 1077646, 22538, 276487, 801031, 45575, 569494,
-        1094038, 30738, 292883, 817423, 1079320, 65561, 47137, 571543, 61847, 1095720, 323625, 848158, 53790, 340006,
-        55590, 1126822, 71714, 98350, 100526, 880942, 86574, 88095, 587935, 1112479, 114727, 604327, 117159, 111143,
-        96438, 620719, 897334, 1159599, 127026, 105007, 651454, 1175998, 120890, 374839, 899383, 129591, 653503, 1178047,
+        2048, 274438, 798982, 4614, 16387, 32777, 14353, 51224, 291079, 801038, 1063310, 28807, 21006, 22550,
+        569494, 1094038, 38930, 65566, 585886, 30753, 1110430, 55322, 292904, 1079567, 817193, 98327, 100503, 833815,
+        78359, 602278, 63544, 117158, 1126559, 587810, 72095, 356398, 619039, 1143214, 110634, 88246, 897334, 102966,
+        127027, 651454, 80318, 119358, 120999, 604583, 96807, 620719, 899631, 391599, 374839, 1161527, 915519, 1177919,
         3934080, 3934080, 3934080, 3934080, 3934080, 3934080, 3934080, 3934080, 3934080, 3934080, 3934080, 3934080, 3934080, 3934080,
         3934080, 3934080, 3934080, 3934080, 3934080, 3934080, 3934080, 3934080, 3934080, 3934080, 3934080, 3934080, 3934080, 3934080,
         3934080, 3934080, 3934080, 3934080, 3934080, 3934080, 3934080, 3934080, 3934080, 3934080, 3934080, 3934080,
     ),
     (3, 1): (
-        2048, 18440, 270340, 794884, 12804, 32902, 798982, 35334, 24578, 549004, 811011, 29196, 553102, 10638,
-        21006, 534661, 1059205, 14356, 303115, 565383, 801031, 1063316, 45588, 307213, 569485, 831757, 1094029, 30738,
-        1075343, 555027, 49551, 51727, 65557, 67733, 47381, 1091989, 57495, 571548, 844060, 1106327, 61480, 74263,
-        323748, 860452, 84516, 848158, 53790, 340006, 864550, 55846, 90146, 614572, 1139116, 94243, 356400, 880942,
-        321565, 584238, 86429, 64029, 337957, 862501, 1124511, 88351, 1112479, 100391, 604327, 106919, 92711, 368813,
-        631085, 879028, 1141300, 114742, 96438, 620719, 117046, 883126, 1159228, 1145020, 127026, 909628, 1171646, 651315,
-        1175998, 120890, 370741, 895285, 113205, 637111, 899133, 1161405, 911677, 129597, 653503, 1178047,
+        2048, 270340, 794884, 1056774, 536710, 1061254, 4104, 18435, 34832, 272389, 534552, 14725, 1058841, 24711,
+        286983, 549255, 811527, 1073166, 41102, 303374, 565646, 21006, 827414, 23060, 57494, 319766, 582038, 37398,
+        843806, 39452, 323597, 289054, 550944, 67998, 1110413, 1075226, 30741, 55439, 555157, 567336, 1079701, 1091625,
+        47503, 336023, 98340, 598295, 1122724, 833565, 321585, 584215, 78237, 340509, 602156, 864428, 63544, 326182,
+        876844, 1138975, 849972, 630964, 117279, 356398, 1155508, 69934, 1143214, 372790, 634915, 123318, 385590, 909628,
+        86588, 337957, 127269, 389541, 913451, 1124670, 79917, 354878, 102567, 878893, 604717, 1128871, 358447, 620595,
+        370741, 895285, 883253, 119343, 120887, 125111, 649405, 1173949, 899383, 129591, 653503, 1178047,
     ),
 }
 
@@ -103,7 +103,7 @@
            lens_ref, slopes_ref, x_hbm, wqkv_hbm, wout_hbm, wup_hbm, wdown_hbm,
            g1_ref, s1_ref, bqkv_ref, bo_ref, g2_ref, s2_ref, bup_ref, bd_ref,
            out_hbm,
-           wqkv, wout, wup, wdown, xbuf, in1, in2, part, a_ref, u_ref, q_ref, kv_ref, ctx, ctxb,
+           wqkv, wout, wup, wdown, xbuf, in1, in2, part, a_ref, u_ref, q_ref, kv_ref, ctx, ctxb, bq_ref,
            wq_sem, wo_sem, wu_sem, wd_sem, x_sem, in1_sem, in2_sem, s1_sem, s2_sem, f_sem, o_sem):
     tp = lax.axis_index('tp')
     pp = lax.axis_index('pp')
@@ -169,6 +169,18 @@
     mine = [(((pp == stage) & (inner if role else outer)).astype(jnp.int32), words) for (stage, role), words in TABLES.items()]
     table = [sum(sel * words[j] for sel, words in mine) for j in range(len(TABLES[0, 0]))]
     pl.semaphore_wait(barrier, sum(cond.astype(jnp.int32) for cond, _ in links))
+
+    width = heads_loc * head_dim
+    lane = lax.broadcasted_iota(jnp.int32, (head_dim, width), 1)
+    row = lax.broadcasted_iota(jnp.int32, (head_dim, width), 0)
+    pick = functools.reduce(jnp.logical_or, [lane == row + head_dim * h for h in range(heads_loc)])
+    pick = pick.astype(jnp.float32).astype(jnp.bfloat16)
+    low = lax.broadcasted_iota(jnp.int32, (heads_loc, width), 0) * head_dim
+    lane = lax.broadcasted_iota(jnp.int32, (heads_loc, width), 1)
+    own = (lane >= low) & (lane < low + head_dim)
+    for c in range(3):
+        spread = jnp.dot(bqkv_ref[0, c], pick, preferred_element_type=jnp.float32)
+        bq_ref[c:c + 1, :] = jnp.sum(jnp.where(own, spread, 0.0), axis=0, keepdims=True)
 
     def part_copy(k, c):
         return pltpu.make_async_remote_copy(
@@ -274,7 +286,7 @@
             def _(c=c):
                 wq_copy(c).wait()
             acc = jnp.dot(a_ref[...], wqkv[c], preferred_element_type=jnp.float32)
-            acc = (acc + bqkv_ref[c:c + 1, :].astype(jnp.float32)).astype(jnp.bfloat16)
+            acc = (acc + bq_ref[c:c + 1, :]).astype(jnp.bfloat16)
             if c == 0:
                 q_ref[...] = acc
             else:
@@ -351,9 +363,15 @@
                     r2(u, a, c)
         return lax.div(word, 2048)
 
-    @pl.loop(0, len(TABLES[0, 0]))
+    def two_steps(_, group):
+        lax.fori_loop(0, 2, step, group[0])
+        return group[1:] + group[:1]
+
+    @pl.loop(0, len(table) // 8)
     def _(t):
-        lax.fori_loop(0, 2, step, sum((t == j).astype(jnp.int32) * word for j, word in enumerate(table)))
+        hits = [(t == i).astype(jnp.int32) for i in range(len(table) // 8)]
+        group = tuple(sum(hit * table[8 * i + j] for i, hit in enumerate(hits)) for j in range(8))
+        lax.fori_loop(0, 8, two_steps, group)
 
     @pl.loop(0, 2 * units)
     def _(k):
@@ -414,6 +432,7 @@
                 pltpu.VMEM((2, seq_n, width_loc), bf),
                 pltpu.VMEM((TOK, width_loc), jnp.float32),
                 pltpu.VMEM((TOK, width_loc), bf),
+                pltpu.VMEM((3, width_loc), jnp.float32),
                 dma((3,)), dma((nw,)), dma((nu,)), dma((nw,)),
                 dma((units, nc)), dma((2 * units, nc)), dma((2 * units, nc)),
                 dma((2 * units, nc)), dma((2 * units, nc)), dma((units, nc)), dma((units, nc)),
@@ -425,7 +444,7 @@
             seq_lens.reshape(micro_n), slopes,
             x_in.reshape(micro_n, seq_n, model_n),
             jnp.transpose(w_qkv[0], (1, 0, 2)), w_out[0], w_up[0], w_down[0],
-            ln1_gain, ln1_shift, b_qkv.reshape(3, width_loc), b_out, ln2_gain, ln2_shift, b_up, b_down,
+            ln1_gain, ln1_shift, b_qkv, b_out, ln2_gain, ln2_shift, b_up, b_down,
         )
         return out.reshape(1, micro_n, batch_n, seq_n, model_n)
 

time: 335 us -> 342 us (1.021)
  Pallas kernels: 330 us -> 339 us
    pallas_call x1, Pallas kernels: 330 us -> 339 us  [per_device(): pl.pallas_call(body, out_shape=jax.ShapeDtypeStruct((micro_n, seq_n, mode...]
where the time goes in v4:
time: 342 us
  Pallas kernels  339 us (99%)
    pallas_call x1, Pallas kernels, per_device(): pl.pallas_call(body, out_shape=jax.ShapeDtypeStruct((micro_n, seq_n, mode...  339 us

profile of v4, /device:TPU:5, one launch (start us, length us, event | category | flops | bytes accessed | tf_op | source)
XLA Modules:
  0.0 342.2 jit_solution(18082712567593083666)
XLA Ops:
  0.0 338.8 %stages.1 = bf16[4,128,2560]{2,1,0:T(8,128)(2,1)} custom-call(s32[4]{0:T(128)} %bitcast.17, f32[32]{0:T(128)} %constant.2.clone.slopes_ref, bf16[4,128,2560]{2,1,0:T(8,128)(2,1)} %bitcast.16, bf16[3,2560,640]{2,1,0:T(8,128)(2,1)} %bitcast.14, bf16[640,2560]{1,0:T(8,128)(2,1)} %bitcast.15, bf16[2560,2560]{1,0:T(8,128)(2,1)} %bitcast.11, ...), custom_call_target="tpu_custom_call" | custom-call | tf_op jit(solution)/shard_map/stages/pallas_call | solution.py:415
  338.8 3.4 copy.18

commit v5 on v2

--- a/solution.py
+++ b/solution.py
@@ -26,7 +26,7 @@
            lens_ref, slopes_ref, x_hbm, wqkv_hbm, wout_hbm, wup_hbm, wdown_hbm,
            g1_ref, s1_ref, bqkv_ref, bo_ref, g2_ref, s2_ref, bup_ref, bd_ref,
            out_hbm,
-           wqkv, wout, wup, wdown, xbuf, in1, in2, part, a_ref, u_ref, qkv, ctx, ctxb,
+           wqkv, wout, wup, wdown, xbuf, in1, in2, part, a_ref, u_ref, qkv, ctx, ctxb, bq_ref,
            wq_sem, wo_sem, wu_sem, wd_sem, x_sem, in1_sem, in2_sem, s1_sem, s2_sem, f_sem, o_sem):
     tp = lax.axis_index('tp')
     pp = lax.axis_index('pp')
@@ -83,6 +83,18 @@
         def _(dev=dev):
             pl.semaphore_signal(barrier, inc=1, device_id=dev, device_id_type=MESH)
     pl.semaphore_wait(barrier, sum(cond.astype(jnp.int32) for cond, _ in links))
+
+    width = heads_loc * head_dim
+    lane = lax.broadcasted_iota(jnp.int32, (head_dim, width), 1)
+    row = lax.broadcasted_iota(jnp.int32, (head_dim, width), 0)
+    pick = functools.reduce(jnp.logical_or, [lane == row + head_dim * h for h in range(heads_loc)])
+    pick = pick.astype(jnp.float32).astype(jnp.bfloat16)
+    low = lax.broadcasted_iota(jnp.int32, (heads_loc, width), 0) * head_dim
+    lane = lax.broadcasted_iota(jnp.int32, (heads_loc, width), 1)
+    own = (lane >= low) & (lane < low + head_dim)
+    for c in range(3):
+        spread = jnp.dot(bqkv_ref[0, c], pick, preferred_element_type=jnp.float32)
+        bq_ref[c:c + 1, :] = jnp.sum(jnp.where(own, spread, 0.0), axis=0, keepdims=True)
 
     def part_copy(k, c):
         return pltpu.make_async_remote_copy(
@@ -186,7 +198,7 @@
             def _(c=c):
                 wq_copy(c).wait()
             acc = jnp.dot(a_ref[...], wqkv[c], preferred_element_type=jnp.float32)
-            qkv[c] = (acc + bqkv_ref[c:c + 1, :].astype(jnp.float32)).astype(jnp.bfloat16)
+            qkv[c] = (acc + bq_ref[c:c + 1, :]).astype(jnp.bfloat16)
         attention(s)
         own_partial(s, 0, ctxb, wout, wo_copy)
 
@@ -203,40 +215,51 @@
             u_ref[:, cols(c, WC)] = t.astype(jnp.bfloat16)
         own_partial(s, 1, u_ref, wdown, wd_copy)
 
-    def r1(s, a):
-        k = 2 * s + a
-
-        @pl.when(inner)
-        def _():
-            @pl.loop(0, nc)
-            def _(c):
-                part_copy(k, c).wait_recv()
-                part[a, c] = (part[a, c].astype(jnp.float32) + in1[k, c].astype(jnp.float32)).astype(jnp.bfloat16)
-                sum_copy(k, c).start()
-
-    def r2(s, a):
+    lag = 6
+
+    def reduce(s, a):
         k = 2 * s + a
         bias = bo_ref if a == 0 else bd_ref
 
-        @pl.loop(0, nc)
-        def _(c):
-            @pl.when(inner)
-            def _():
-                sum_copy(k, c).wait_recv()
-                resid = xbuf[s, c] if a == 0 else in1[2 * s, c]
-                total = part[a, c].astype(jnp.float32) + in2[k, c].astype(jnp.float32)
-                in1[k, c] = (resid.astype(jnp.float32) + total + bias[:, cols(c)].astype(jnp.float32)).astype(jnp.bfloat16)
-                res_copy(k, c).start()
-
-            @pl.when(outer)
-            def _():
-                part_copy(k, c).wait_recv()
+        def forward(c):
+            part_copy(k, c).wait_recv()
+            part[a, c] = (part[a, c].astype(jnp.float32) + in1[k, c].astype(jnp.float32)).astype(jnp.bfloat16)
+            sum_copy(k, c).start()
+
+        def leave(c):
             if a == 1:
                 @pl.when(sends)
                 def _():
                     fwd_copy(s, c).start()
                 out_copy(s, c).start()
 
+        def finish(c):
+            sum_copy(k, c).wait_recv()
+            resid = xbuf[s, c] if a == 0 else in1[2 * s, c]
+            total = part[a, c].astype(jnp.float32) + in2[k, c].astype(jnp.float32)
+            in1[k, c] = (resid.astype(jnp.float32) + total + bias[:, cols(c)].astype(jnp.float32)).astype(jnp.bfloat16)
+            res_copy(k, c).start()
+            leave(c)
+
+        @pl.when(inner)
+        def _():
+            @pl.loop(0, nc + lag)
+            def _(i):
+                @pl.when(i < nc)
+                def _():
+                    forward(i)
+
+                @pl.when(i >= lag)
+                def _():
+                    finish(i - lag)
+
+        @pl.when(outer)
+        def _():
+            @pl.loop(0, nc)
+            def _(c):
+                part_copy(k, c).wait_recv()
+                leave(c)
+
     @pl.loop(0, micro_n + 1)
     def _(s):
         @pl.when(s < micro_n)
@@ -245,13 +268,11 @@
 
         @pl.when(s > 0)
         def _():
-            r1(s - 1, 1)
-            r2(s - 1, 1)
+            reduce(s - 1, 1)
 
         @pl.when(s < micro_n)
         def _():
-            r1(s, 0)
-            r2(s, 0)
+            reduce(s, 0)
             p2(s)
 
     last = micro_n - 1
@@ -314,6 +335,7 @@
                 pltpu.VMEM((3, seq_n, width_loc), bf),
                 pltpu.VMEM((seq_n, width_loc), jnp.float32),
                 pltpu.VMEM((seq_n, width_loc), bf),
+                pltpu.VMEM((3, width_loc), jnp.float32),
                 dma((3,)), dma((nw,)), dma((nu,)), dma((nw,)),
                 dma((micro_n, nc)), dma((2 * micro_n, nc)), dma((2 * micro_n, nc)),
                 dma((2 * micro_n, nc)), dma((2 * micro_n, nc)), dma((micro_n, nc)), dma((micro_n, nc)),
@@ -325,7 +347,7 @@
             seq_lens.reshape(micro_n), slopes,
             x_in.reshape(micro_n, seq_n, model_n),
             jnp.transpose(w_qkv[0], (1, 0, 2)), w_out[0], w_up[0], w_down[0],
-            ln1_gain, ln1_shift, b_qkv.reshape(3, width_loc), b_out, ln2_gain, ln2_shift, b_up, b_down,
+            ln1_gain, ln1_shift, b_qkv, b_out, ln2_gain, ln2_shift, b_up, b_down,
         )
         return out.reshape(1, micro_n, batch_n, seq_n, model_n)
 

time: 319 us -> 307 us (0.962)
  Pallas kernels: 313 us -> 303 us
    pallas_call x1, Pallas kernels: 313 us -> 303 us  [per_device(): pl.pallas_call(body, out_shape=jax.ShapeDtypeStruct((micro_n, seq_n, mode...]
where the time goes in v5:
time: 307 us
  Pallas kernels  303 us (99%)
  local copies, waits for them, and re-layouts  3.4 us (1%)
    pallas_call x1, Pallas kernels, per_device(): pl.pallas_call(body, out_shape=jax.ShapeDtypeStruct((micro_n, seq_n, mode...  303 us

profile of v5, /device:TPU:5, one launch (start us, length us, event | category | flops | bytes accessed | tf_op | source)
XLA Modules:
  0.0 306.5 jit_solution(15145916277387575436)
XLA Ops:
  0.0 303.1 %stages.1 = bf16[4,128,2560]{2,1,0:T(8,128)(2,1)} custom-call(s32[4]{0:T(128)} %bitcast.17, f32[32]{0:T(128)} %constant.2.clone.slopes_ref, bf16[4,128,2560]{2,1,0:T(8,128)(2,1)} %bitcast.16, bf16[3,2560,640]{2,1,0:T(8,128)(2,1)} %bitcast.14, bf16[640,2560]{1,0:T(8,128)(2,1)} %bitcast.15, bf16[2560,2560]{1,0:T(8,128)(2,1)} %bitcast.11, ...), custom_call_target="tpu_custom_call" | custom-call | tf_op jit(solution)/shard_map/stages/pallas_call | solution.py:319
  303.1 3.4 %copy.18 = bf16[1,4,1,128,2560]{4,3,2,1,0:T(8,128)(2,1)} copy(bf16[1,4,1,128,2560]{4,3,2,1,0:T(8,128)(2,1)} %bitcast.13) | data formatting | bytes 5242880

commit v6 on v5

--- a/solution.py
+++ b/solution.py
@@ -215,64 +215,103 @@
             u_ref[:, cols(c, WC)] = t.astype(jnp.bfloat16)
         own_partial(s, 1, u_ref, wdown, wd_copy)
 
-    lag = 6
-
-    def reduce(s, a):
+    lag = 5
+    early = 4
+
+    def forward(s, a, c):
+        k = 2 * s + a
+        part_copy(k, c).wait_recv()
+        part[a, c] = (part[a, c].astype(jnp.float32) + in1[k, c].astype(jnp.float32)).astype(jnp.bfloat16)
+        sum_copy(k, c).start()
+
+    def leave(s, a, c):
+        if a == 1:
+            @pl.when(sends)
+            def _():
+                fwd_copy(s, c).start()
+            out_copy(s, c).start()
+
+    def finish(s, a, c):
         k = 2 * s + a
         bias = bo_ref if a == 0 else bd_ref
-
-        def forward(c):
-            part_copy(k, c).wait_recv()
-            part[a, c] = (part[a, c].astype(jnp.float32) + in1[k, c].astype(jnp.float32)).astype(jnp.bfloat16)
-            sum_copy(k, c).start()
-
-        def leave(c):
-            if a == 1:
-                @pl.when(sends)
+        sum_copy(k, c).wait_recv()
+        resid = xbuf[s, c] if a == 0 else in1[2 * s, c]
+        total = part[a, c].astype(jnp.float32) + in2[k, c].astype(jnp.float32)
+        in1[k, c] = (resid.astype(jnp.float32) + total + bias[:, cols(c)].astype(jnp.float32)).astype(jnp.bfloat16)
+        res_copy(k, c).start()
+        leave(s, a, c)
+
+    def reduce_inner(s, had, more):
+        @pl.when(had)
+        def _():
+            @pl.loop(0, nc - 1)
+            def _(i):
+                forward(s - 1, 1, i)
+
+                @pl.when(i >= lag)
                 def _():
-                    fwd_copy(s, c).start()
-                out_copy(s, c).start()
-
-        def finish(c):
-            sum_copy(k, c).wait_recv()
-            resid = xbuf[s, c] if a == 0 else in1[2 * s, c]
-            total = part[a, c].astype(jnp.float32) + in2[k, c].astype(jnp.float32)
-            in1[k, c] = (resid.astype(jnp.float32) + total + bias[:, cols(c)].astype(jnp.float32)).astype(jnp.bfloat16)
-            res_copy(k, c).start()
-            leave(c)
-
-        @pl.when(inner)
-        def _():
-            @pl.loop(0, nc + lag)
+                    finish(s - 1, 1, i - lag)
+            forward(s - 1, 1, nc - 1)
+            finish(s - 1, 1, nc - 1 - lag)
+
+        @pl.loop(0, early)
+        def _(i):
+            @pl.when(more)
+            def _():
+                forward(s, 0, i)
+
+            @pl.when(had)
+            def _():
+                for j in range(2):
+                    c = nc - lag + 2 * i + j
+
+                    @pl.when(c < nc)
+                    def _(c=c):
+                        finish(s - 1, 1, c)
+
+        @pl.when(more)
+        def _():
+            @pl.loop(early, nc + lag)
             def _(i):
                 @pl.when(i < nc)
                 def _():
-                    forward(i)
+                    forward(s, 0, i)
 
                 @pl.when(i >= lag)
                 def _():
-                    finish(i - lag)
-
-        @pl.when(outer)
-        def _():
-            @pl.loop(0, nc)
-            def _(c):
-                part_copy(k, c).wait_recv()
-                leave(c)
+                    finish(s, 0, i - lag)
+
+    def reduce_outer(s, a):
+        @pl.loop(0, nc)
+        def _(c):
+            part_copy(2 * s + a, c).wait_recv()
+            leave(s, a, c)
 
     @pl.loop(0, micro_n + 1)
     def _(s):
-        @pl.when(s < micro_n)
+        had = s > 0
+        more = s < micro_n
+
+        @pl.when(more)
         def _():
             p1(s)
 
-        @pl.when(s > 0)
-        def _():
-            reduce(s - 1, 1)
-
-        @pl.when(s < micro_n)
-        def _():
-            reduce(s, 0)
+        @pl.when(inner)
+        def _():
+            reduce_inner(s, had, more)
+
+        @pl.when(outer)
+        def _():
+            @pl.when(had)
+            def _():
+                reduce_outer(s - 1, 1)
+
+            @pl.when(more)
+            def _():
+                reduce_outer(s, 0)
+
+        @pl.when(more)
+        def _():
             p2(s)
 
     last = micro_n - 1

time: 307 us -> 296 us (0.964)
  Pallas kernels: 303 us -> 292 us
    pallas_call x1, Pallas kernels: 303 us -> 292 us  [per_device(): pl.pallas_call(body, out_shape=jax.ShapeDtypeStruct((micro_n, seq_n, mode...]
where the time goes in v6:
time: 296 us
  Pallas kernels  292 us (99%)
  local copies, waits for them, and re-layouts  3.4 us (1%)
    pallas_call x1, Pallas kernels, per_device(): pl.pallas_call(body, out_shape=jax.ShapeDtypeStruct((micro_n, seq_n, mode...  292 us

profile of v6, /device:TPU:5, one launch (start us, length us, event | category | flops | bytes accessed | tf_op | source)
XLA Modules:
  0.0 295.9 jit_solution(14841390018032124892)
XLA Ops:
  0.0 292.5 %stages.1 = bf16[4,128,2560]{2,1,0:T(8,128)(2,1)} custom-call(s32[4]{0:T(128)} %bitcast.17, f32[32]{0:T(128)} %constant.2.clone.slopes_ref, bf16[4,128,2560]{2,1,0:T(8,128)(2,1)} %bitcast.16, bf16[3,2560,640]{2,1,0:T(8,128)(2,1)} %bitcast.14, bf16[640,2560]{1,0:T(8,128)(2,1)} %bitcast.15, bf16[2560,2560]{1,0:T(8,128)(2,1)} %bitcast.11, ...), custom_call_target="tpu_custom_call" | custom-call | tf_op jit(solution)/shard_map/stages/pallas_call | solution.py:358
  292.5 3.4 %copy.18 = bf16[1,4,1,128,2560]{4,3,2,1,0:T(8,128)(2,1)} copy(bf16[1,4,1,128,2560]{4,3,2,1,0:T(8,128)(2,1)} %bitcast.13) | data formatting | bytes 5242880
